TPU v7x, 32 devices: a 4x4x1 block of a 4x4x8 slice. The times are simulated.
32 devices in a mesh: dp: 1 (over z), vp: 32 (over y, x, core).
Axes of the slice: x: 4, y: 4, z: 1, core: 2. Of those that a mesh axis runs over, the one named last changes fastest.
The devices are a block of a 4x4x8 slice.
Arguments:
- hidden: bfloat16 [256, 32, 2048], P('vp', 'dp')
- norm_gain: float32 [2048], replicated
- norm_bias: float32 [2048], replicated
- w_out: bfloat16 [2048, 49152], P(None, 'vp')
- labels: int32 [256, 32], P('vp', 'dp')
- loss_mask: float32 [256, 32], P('vp', 'dp')
Outputs:
- output 1: float32 [1], P('dp')
- output 2: bfloat16 [256, 32, 2048], P('vp', 'dp')
- output 3: float32 [2048, 49152], P('dp', 'vp')
- output 4: float32 [2048], P('dp')
- output 5: float32 [2048], P('dp')
All inputs are finite; a program needn't handle non-finite values.
Results may differ from a plain program's by a relative error of at most 0.001.
Values are sent between devices in bfloat16 or wider.
A program may use at most 768 MiB of HBM per device.

v0:
```python
import jax
import jax.numpy as jnp
from jax import lax
from jax.sharding import PartitionSpec as P

NORM_EPS = 1e-5


def norm_forward(hidden, norm_gain, norm_bias):
    x_float = hidden.astype(jnp.float32)
    tok_mean = jnp.mean(x_float, axis=-1, keepdims=True)
    centered = x_float - tok_mean
    inv_std = lax.rsqrt(jnp.mean(centered * centered, axis=-1, keepdims=True) + NORM_EPS)
    normed = centered * inv_std
    h_bf = (normed * (1.0 + norm_gain) + norm_bias).astype(jnp.bfloat16)
    return h_bf, normed, inv_std


def norm_backward(grad_h, normed, inv_std, norm_gain):
    scaled = grad_h * (1.0 + norm_gain)
    centered_grad = scaled - jnp.mean(scaled, axis=-1, keepdims=True)
    return (inv_std * (centered_grad - normed * jnp.mean(scaled * normed, axis=-1, keepdims=True))).astype(jnp.bfloat16)


def solution(mesh):
    def per_device(hidden, norm_gain, norm_bias, w_blk, labels, loss_mask):
        h_bf, normed, inv_std = norm_forward(hidden, norm_gain, norm_bias)
        h_all = lax.all_gather(h_bf, "vp", axis=0, tiled=True)
        labels_all = lax.all_gather(labels, "vp", axis=0, tiled=True)
        mask_all = lax.all_gather(loss_mask, "vp", axis=0, tiled=True)
        vocab_local = w_blk.shape[1]
        col_start = lax.axis_index("vp") * vocab_local
        logits = jnp.einsum("sbd,dv->sbv", h_all, w_blk, preferred_element_type=jnp.float32)
        row_max = lax.pmax(jnp.max(logits, axis=-1), "vp")
        exp_shift = jnp.exp(logits - row_max[:, :, None])
        col_ids = col_start + lax.broadcasted_iota(jnp.int32, (1, 1, vocab_local), 2)
        is_label = col_ids == labels_all[:, :, None]
        sum_exp = lax.psum(jnp.sum(exp_shift, axis=-1), "vp")
        target = lax.psum(jnp.sum(jnp.where(is_label, logits, 0.0), axis=-1), "vp")
        mask_total = jnp.sum(mask_all)
        tok_loss = row_max + jnp.log(sum_exp) - target
        loss = jnp.sum(mask_all * tok_loss) / mask_total
        prob_soft = exp_shift / sum_exp[:, :, None]
        tok_weight = mask_all / mask_total
        grad_logits = (jnp.where(is_label, prob_soft - 1.0, prob_soft) * tok_weight[:, :, None]).astype(jnp.bfloat16)
        grad_w = jnp.einsum("sbd,sbv->dv", h_all, grad_logits, preferred_element_type=jnp.float32)
        grad_h_part = jnp.einsum("sbv,dv->sbd", grad_logits, w_blk, preferred_element_type=jnp.float32)
        grad_h = lax.psum_scatter(grad_h_part, "vp", scatter_dimension=0, tiled=True)
        grad_gain = lax.psum(jnp.sum(grad_h * normed, axis=(0, 1)), "vp")
        grad_bias = lax.psum(jnp.sum(grad_h, axis=(0, 1)), "vp")
        grad_x = norm_backward(grad_h, normed, inv_std, norm_gain)
        return loss.reshape(1), grad_x, grad_w, grad_gain, grad_bias

    tok_spec = P("vp", "dp")
    return jax.shard_map(
        per_device,
        mesh=mesh,
        in_specs=(P("vp", "dp", None), P(None), P(None), P(None, "vp"), tok_spec, tok_spec),
        out_specs=(P("dp"), P("vp", "dp", None), P("dp", "vp"), P("dp"), P("dp")),
        check_vma=False,
    )
```

profile of v0, /device:TPU:97, one launch (start us, length us, event | category | flops | bytes accessed | tf_op | source)
XLA Modules:
  0.0 709.6 jit_solution(1551049626285451909)
XLA Ops:
  7.2 0.1 all-gather.2.cloned.1.call-start
  7.2 0.7 broadcast_add_fusion
  7.9 0.0 copy-start.7
  7.9 1.9 convert_reduce_fusion
  9.9 0.0 copy-start.1
  9.9 2.4 fusion.21
  12.3 0.0 copy-done.7
  12.3 0.0 copy-done.1
  12.3 0.0 copy-start.5
  12.3 0.6 copy-done.5
  12.9 3.0 fusion.15
  15.9 0.1 all-gather.2.cloned.1.call-update
  16.0 0.1 reduce-scatter.2.cloned.1.call-start
  16.1 33.5 %all_gather.9 = f32[256,32]{1,0:T(8,128)S(1)} all-gather(f32[8,32]{1,0:T(8,128)} %param.11), channel_id=1, replica_groups=mesh['dp'=1,'vp'=32] {'vp'}, dimensions={0}, use_global_device_ids=true | all-gather | bytes 33792 | tf_op jit(solution)/shard_map/all_gather | solution.py:30
  49.5 0.1 copy.28
  49.6 0.0 copy-start.3
  49.6 0.6 reduce_sum.95
  50.2 33.4 %all_gather.11 = s32[256,32]{1,0:T(8,128)S(1)} all-gather(s32[8,32]{1,0:T(8,128)} %param.10), channel_id=1, replica_groups=mesh['dp'=1,'vp'=32] {'vp'}, dimensions={0}, use_global_device_ids=true | all-gather | bytes 33792 | tf_op jit(solution)/shard_map/all_gather | solution.py:29
  83.7 0.1 copy.27
  83.7 0.7 broadcast_divide_fusion
  84.4 45.9 %all-gather.2.cloned.1.call-done = bf16[256,32,2048]{2,0,1:T(8,128)(2,1)} async-done(((bf16[8,32,2048]{2,0,1:T(8,128)(2,1)}), bf16[256,32,2048]{2,0,1:T(8,128)(2,1)}) %all-gather.2.cloned.1.call-update) | async-done | bytes 33554448 | tf_op jit(solution)/shard_map/all_gather | solution.py:28
  130.3 60.6 %fusion.24 = (f32[256,32]{0,1:T(8,128)S(1)}, f32[256,32,1536]{2,0,1:T(8,128)}) fusion(bf16[256,32,2048]{2,0,1:T(8,128)(2,1)} %all-gather.2.cloned.1.call-done, bf16[2048,1536]{1,0:T(8,128)(2,1)} %param.9), kind=kOutput, calls=%fused_computation.37 | convolution fusion | flops 51552182272 | bytes 90210304 | tf_op jit(solution)/shard_map/sbd,dv->sbv/dot_general | solution.py:33
  190.9 0.0 copy-done.3
  190.9 44.8 %pmax.7 = f32[256,32]{0,1:T(8,128)S(1)} all-reduce(f32[256,32]{0,1:T(8,128)S(1)} %get-tuple-element.34), channel_id=1, replica_groups=mesh['dp'=1,'vp'=32] {'vp'}, use_global_device_ids=true, to_apply=%region_3.0 | all-reduce | flops 8192 | bytes 65536 | tf_op jit(solution)/shard_map/pmax | solution.py:34
  235.6 17.1 %fusion.3 = (f32[256,32]{0,1:T(8,128)S(1)}, f32[256,32]{0,1:T(8,128)}) fusion(f32[256,32,1536]{2,0,1:T(8,128)} %get-tuple-element.35, f32[256,32]{0,1:T(8,128)S(1)} %pmax.7, s32[256,32]{0,1:T(8,128)S(1)} %copy.27, s32[1536]{0:T(1024)S(1)} %iota_add_fusion), kind=kLoop, calls=%fused_computation.6 | loop fusion | flops 62898176 | bytes 50468864 | tf_op jit(solution)/shard_map/reduce_sum | solution.py:38
  252.8 44.8 %psum.28 = f32[256,32]{0,1:T(8,128)S(1)} all-reduce(f32[256,32]{0,1:T(8,128)S(1)} %get-tuple-element.25), channel_id=1, replica_groups=mesh['dp'=1,'vp'=32] {'vp'}, use_global_device_ids=true, to_apply=%region_5.0 | all-reduce | flops 8192 | bytes 65536 | tf_op jit(solution)/shard_map/psum | solution.py:38
  297.6 66.2 %fusion.4 = f32[256,32,2048]{2,0,1:T(8,128)} fusion(bf16[2048,1536]{1,0:T(8,128)(2,1)} %param.9, f32[256,32,1536]{2,0,1:T(8,128)} %get-tuple-element.35, f32[256,32]{0,1:T(8,128)S(1)} %broadcast_divide_fusion, f32[256,32]{0,1:T(8,128)S(1)} %psum.28, s32[256,32]{0,1:T(8,128)S(1)} %copy.27, s32[1536]{0:T(1024)S(1)} %iota_add_fusion, f32[256,32]{0,1:T(8,128)S(1)} %pmax.7), kind=kOutput, calls=%fused_computation.8 | convolution fusion | flops 51627687936 | bytes 123869184 | tf_op jit(solution)/shard_map/sbv,dv->sbd/dot_general | solution.py:47
  363.8 0.1 reduce-scatter.2.cloned.1.call-update
  363.8 0.0 copy-start
  363.8 0.0 copy-start.2
  363.9 0.0 copy-start.6
  363.9 0.0 copy-start.8
  363.9 0.0 copy-start.9
  363.9 0.0 copy-start.4
  363.9 73.5 %convolution_bitcast_fusion = f32[2048,1536]{1,0:T(8,128)} fusion(bf16[256,32,2048]{2,0,1:T(8,128)(2,1)} %all-gather.2.cloned.1.call-done, f32[256,32,1536]{2,0,1:T(8,128)} %get-tuple-element.35, f32[256,32]{0,1:T(8,128)S(1)} %broadcast_divide_fusion, f32[256,32]{0,1:T(8,128)S(1)} %psum.28, s32[256,32]{0,1:T(8,128)S(1)} %copy.27, ...), kind=kOutput, calls=%fused_computation.7 | convolution fusion | flops 51627687936 | bytes 96606208 | tf_op jit(solution)/shard_map/sbd,sbv->dv/dot_general | solution.py:46
  437.4 209.3 %reduce-scatter.2.cloned.1.call-done = f32[8,32,2048]{2,0,1:T(8,128)} async-done(((f32[256,32,2048]{2,0,1:T(8,128)}), f32[8,32,2048]{2,0,1:T(8,128)}) %reduce-scatter.2.cloned.1.call-update) | async-done | bytes 2097168 | tf_op jit(solution)/shard_map/reduce_scatter | solution.py:48
  646.7 0.0 copy-done
  646.7 0.0 copy-done.2
  646.7 0.0 copy-done.6
  646.7 0.0 copy-done.8
  646.7 2.9 fusion.20
  649.6 0.0 copy-done.9
  649.7 45.7 %all-reduce = (f32[256,32]{0,1:T(8,128)S(1)}, f32[2048]{0:T(1024)}, f32[2048]{0:T(1024)}) all-reduce(f32[256,32]{0,1:T(8,128)S(1)} %copy-done.9, f32[2048]{0:T(1024)S(1)} %get-tuple-element.27, f32[2048]{0:T(1024)S(1)} %get-tuple-element.30), channel_id=1, replica_groups=mesh['dp'=1,'vp'=32] {'vp'}, use_global_device_ids=true, to_apply=%region_7.8 | all-reduce | flops 12288 | bytes 98304 | tf_op jit(solution)/shard_map/psum | solution.py:39
  695.4 0.0 copy-done.4
  695.4 0.6 multiply_reduce_fusion.1
  697.3 2.8 fusion.19
  700.1 1.5 copy.30
  (4 shorter events, 0.0 us)
Async XLA Ops:
  7.2 123.1 %all-gather.2.cloned.1.call-start = ((), (), s32[]{:S(2)}) async-start(), calls=%async_computation.1 | async-start | bytes 34603008 | tf_op jit(solution)/shard_map/all_gather | solution.py:28
  7.9 4.3 copy-start.7
  9.9 2.4 copy-start.1
  12.3 0.6 copy-start.5
  16.0 630.8 %reduce-scatter.2.cloned.1.call-start = ((), (), s32[]{:S(2)}) async-start(), calls=%async_computation.2 | async-start | bytes 69206016 | tf_op jit(solution)/shard_map/reduce_scatter | solution.py:48
  49.6 141.3 %copy-start.3 = (f32[256,32]{0,1:T(8,128)}, f32[256,32]{0,1:T(8,128)S(1)}, u32[]{:S(2)}) copy-start(f32[256,32]{0,1:T(8,128)S(1)} %copy.28) | copy-start | bytes 98308
  363.8 282.9 %copy-start = (bf16[8,32,2048]{2,1,0:T(8,128)(2,1)S(1)}, bf16[8,32,2048]{2,1,0:T(8,128)(2,1)}, u32[]{:S(2)}) copy-start(bf16[8,32,2048]{2,1,0:T(8,128)(2,1)} %param.6) | copy-start | bytes 3145732
  363.8 282.9 %copy-start.2 = (f32[8,32]{0,1:T(8,128)S(1)}, f32[8,32]{0,1:T(8,128)}, u32[]{:S(2)}) copy-start(f32[8,32]{0,1:T(8,128)} %copy-done.1) | copy-start | bytes 3076
  363.9 282.9 %copy-start.6 = (f32[8,32]{0,1:T(8,128)S(1)}, f32[8,32]{0,1:T(8,128)}, u32[]{:S(2)}) copy-start(f32[8,32]{0,1:T(8,128)} %copy-done.5) | copy-start | bytes 3076
  363.9 282.9 %copy-start.8 = (f32[2048]{0:T(1024)S(1)}, f32[2048]{0:T(1024)}, u32[]{:S(2)}) copy-start(f32[2048]{0:T(1024)} %copy-done.7) | copy-start | bytes 24580
  363.9 285.8 %copy-start.9 = (f32[256,32]{0,1:T(8,128)S(1)}, f32[256,32]{0,1:T(8,128)}, u32[]{:S(2)}) copy-start(f32[256,32]{0,1:T(8,128)} %get-tuple-element.26) | copy-start | bytes 98308
  363.9 331.5 %copy-start.4 = (f32[256,32]{0,1:T(8,128)S(1)}, f32[256,32]{0,1:T(8,128)}, u32[]{:S(2)}) copy-start(f32[256,32]{0,1:T(8,128)} %copy-done.3) | copy-start | bytes 98308
Sparse Core Ops, SparseCore 0:
  16.1 114.1 all-gather.1
  363.9 282.7 reduce-scatter.1
where the time goes:
time: 711 us; the launch traced here: 710 us
  waiting for transfers between devices  255 us (36%)
  blocking collectives  202 us (28%)
  matrix products  200 us (28%)
  other arithmetic  32.8 us (5%)
  between operations  16.7 us (2%)
    reduce_scatter x1, waiting for transfers between devices, per_device(): lax.psum_scatter(grad_h_part, 'vp', scatter_dimension=0, tiled=True)  209 us
    dot_general x1, matrix products, per_device(): jnp.einsum('sbd,sbv->dv', h_all, grad_logits, preferred_element_type=jnp....  73.5 us
    dot_general x1, matrix products, per_device(): jnp.einsum('sbv,dv->sbd', grad_logits, w_blk, preferred_element_type=jnp....  66.2 us
    dot_general x1, matrix products, per_device(): jnp.einsum('sbd,dv->sbv', h_all, w_blk, preferred_element_type=jnp.float32)  60.6 us
    all_gather x1, waiting for transfers between devices, per_device(): h_all = lax.all_gather(h_bf, 'vp', axis=0, tiled=True)  45.9 us
    psum x1, blocking collectives, per_device(): target = lax.psum(jnp.sum(jnp.where(is_label, logits, 0.0), axis=-1), 'vp')  45.7 us
    psum x1, blocking collectives, per_device(): sum_exp = lax.psum(jnp.sum(exp_shift, axis=-1), 'vp')  44.8 us
    pmax x1, blocking collectives, per_device(): row_max = lax.pmax(jnp.max(logits, axis=-1), 'vp')  44.8 us
  transfers between devices with their start and end apart: 2, of which 2 were waited for; matrix products, arithmetic and copies ran while one was open for 11% of the time, Pallas kernels for 0%

commit v1 on v0

v1 whole, which is shorter than its diff:
```python
import functools
import math

import jax
import jax.numpy as jnp
from jax import lax
from jax.experimental import pallas as pl
from jax.experimental.pallas import tpu as pltpu
from jax.sharding import PartitionSpec as P

NORM_EPS = 1e-5
MESH = pl.DeviceIdType.MESH
VMEM_LIMIT = 66_000_000
F32 = jnp.float32
BF16 = jnp.bfloat16


class Rings:
    def __init__(self, n):
        self.n = n
        self.chips = n // 2
        self.side = math.isqrt(self.chips)
        assert self.side * self.side * 2 == n
        self.me = lax.axis_index("vp")
        self.core = lax.rem(self.me, 2)
        chip = lax.div(self.me, 2)
        x, y = lax.rem(chip, self.side), lax.div(chip, self.side)
        k = lax.rem(x + y, self.side)
        self.spot = (y * self.side + k, x * self.side + k)
        self.sibling = self.me + 1 - 2 * self.core
        step = 2 * self.core - 1
        self.s_next = [self.at(c, lax.rem(self.spot[c] + step + self.chips, self.chips), 1 - self.core) for c in range(2)]
        self.x_prev = [self.at(c, lax.rem(self.spot[c] + step + self.chips, self.chips), 1 - self.core) for c in range(2)]

    def at(self, cycle, spot, core):
        q, k = lax.div(spot, self.side), lax.rem(spot, self.side)
        a = lax.rem(k - q + self.side, self.side)
        chip = q * self.side + a if cycle == 0 else a * self.side + q
        return chip * 2 + core

    def owner(self, group, quarter):
        cycle = quarter % 2
        pos = 2 * self.spot[cycle] + self.core
        shift = self.n - group if quarter < 2 else group
        origin = lax.rem(pos + shift + self.n, self.n)
        return self.at(cycle, lax.div(origin, 2), lax.rem(origin, 2))

    def greet(self, wait=True):
        barrier = pltpu.get_barrier_semaphore()
        for other in (self.sibling, *self.s_next):
            pl.semaphore_signal(barrier, inc=1, device_id={"vp": other}, device_id_type=MESH)

    def greeted(self):
        pl.semaphore_wait(pltpu.get_barrier_semaphore(), 3)


def norm_rows(x_rows):
    x = x_rows.astype(F32)
    centered = x - jnp.mean(x, axis=-1, keepdims=True)
    inv_std = lax.rsqrt(jnp.mean(centered * centered, axis=-1, keepdims=True) + NORM_EPS)
    return centered * inv_std, inv_std


def gather_kernel(n, x_ref, gain_ref, bias_ref, w_hbm, h_hbm, z_hbm, lse_ref,
                  w_v, h_all, zbuf, col, w_sem, h_sem, z_sem, send_x, send_s, recv_x, recv_s):
    ring = Rings(n)
    rows, dim = x_ref.shape
    cols = w_v.shape[1]
    half, quart, piece, wide = rows // 2, rows // 4, rows // 8, cols // 2
    xo = pl.multiple_of(half * ring.core, half)
    so = pl.multiple_of(half * (1 - ring.core), half)

    w_copy = pltpu.make_async_copy(w_hbm, w_v, w_sem)
    w_copy.start()
    ring.greet()

    ln_rows = min(32, rows)

    @pl.loop(0, rows // ln_rows)
    def _(b):
        r = pl.ds(pl.multiple_of(b * ln_rows, ln_rows), ln_rows)
        normed, _ = norm_rows(x_ref[r, :])
        h_all[0, r, :] = (normed * (1.0 + gain_ref[...]) + bias_ref[...]).astype(BF16)

    ring.greeted()

    def x_copy(i, c, u):
        r = pl.ds(xo + (c * quart + u * piece), piece)
        return pltpu.make_async_remote_copy(
            src_ref=h_all.at[i, r], dst_ref=h_all.at[i + 1, r],
            send_sem=send_x.at[lax.rem(i, 4), c, u], recv_sem=recv_s.at[i + 1, c, u],
            device_id={"vp": ring.sibling}, device_id_type=MESH)

    def s_copy(i, c, u):
        r = pl.ds(so + (c * quart + u * piece), piece)
        return pltpu.make_async_remote_copy(
            src_ref=h_all.at[i, r], dst_ref=h_all.at[i + 1, r],
            send_sem=send_s.at[lax.rem(i, 4), c, u], recv_sem=recv_x.at[i + 1, c, u],
            device_id={"vp": ring.s_next[c]}, device_id_type=MESH)

    def x_arrived(i, c, u):
        r = pl.ds(xo + (c * quart + u * piece), piece)
        pltpu.make_async_remote_copy(
            src_ref=h_all.at[i, r], dst_ref=h_all.at[i, r],
            send_sem=send_s.at[0, c, u], recv_sem=recv_x.at[i, c, u],
            device_id={"vp": ring.s_next[c]}, device_id_type=MESH).wait_recv()

    def s_arrived(i, c, u):
        r = pl.ds(so + (c * quart + u * piece), piece)
        pltpu.make_async_remote_copy(
            src_ref=h_all.at[i, r], dst_ref=h_all.at[i, r],
            send_sem=send_x.at[0, c, u], recv_sem=recv_s.at[i, c, u],
            device_id={"vp": ring.sibling}, device_id_type=MESH).wait_recv()

    def send(copy, i, c, u):
        @pl.when(i >= 4)
        def _():
            copy(i - 4, c, u).wait_send()
        copy(i, c, u).start()

    def z_out(g):
        return pltpu.make_async_copy(zbuf.at[lax.rem(g, 2)], z_hbm.at[g], z_sem.at[lax.rem(g, 2)])

    def h_out(g):
        return pltpu.make_async_copy(h_all.at[g], h_hbm.at[g], h_sem.at[lax.rem(g, 2)])

    stat_rows = min(32, half)

    def stats(slot, u):
        for b in range(half // stat_rows):
            z = zbuf[slot, pl.ds(u * half + b * stat_rows, stat_rows), :]
            top = jnp.max(z, axis=-1, keepdims=True)
            lse = top + jnp.log(jnp.sum(jnp.exp(z - top), axis=-1, keepdims=True))
            col[pl.ds(b * stat_rows, stat_rows), :] = jnp.broadcast_to(lse, (stat_rows, col.shape[1]))
        return jnp.transpose(col[...])[0:1, :]

    def put(row, g, u):
        for c in range(2):
            q = 2 * u + c
            lse_ref[ring.owner(g, q), :, q * quart:(q + 1) * quart] = row[:, c * quart:(c + 1) * quart]

    def logits(g, u):
        part = slice(u * wide, (u + 1) * wide)
        zbuf[lax.rem(g, 2), :, part] = jnp.dot(h_all[g], w_v[:, part], preferred_element_type=F32)

    zbuf[...] = jnp.zeros_like(zbuf)
    for c in range(2):
        s_copy(0, c, 0).start()
    w_copy.wait()

    @pl.loop(0, n)
    def _(i):
        g = i - 1
        for u in range(2):
            @pl.when(i >= 1)
            def _():
                for c in range(2):
                    x_arrived(i, c, u)

            @pl.when(i < n - 1)
            def _():
                for c in range(2):
                    send(x_copy, i, c, u)

            j = i + u

            @pl.when((j >= 1) & (j < n))
            def _():
                for c in range(2):
                    s_arrived(j, c, 1 - u)

            @pl.when(j < n - 1)
            def _():
                for c in range(2):
                    send(s_copy, j, c, 1 - u)

            @pl.when(i >= 1)
            def _():
                if u == 0:
                    @pl.when(g >= 2)
                    def _():
                        z_out(g - 2).wait()
                        h_out(g - 2).wait()
                    h_out(g).start()
                logits(g, u)
                row = stats(lax.rem(g + 1, 2), u)
                put(row, lax.max(g - 1, 0), u)
                if u == 1:
                    z_out(g).start()

    last = n - 1
    z_out(last - 2).wait()
    h_out(last - 2).wait()
    h_out(last).start()
    for u in range(2):
        logits(last, u)
        put(stats(lax.rem(last + 1, 2), u), last - 1, u)
    z_out(last).start()
    for u in range(2):
        put(stats(last % 2, u), last, u)
    for g in (last - 1, last):
        z_out(g).wait()
        h_out(g).wait()
    for i in range(n - 5, n - 1):
        for c in range(2):
            for u in range(2):
                x_copy(i, c, u).wait_send()
                s_copy(i, c, u).wait_send()


def gather_logits(n, x, gain, bias, w):
    rows, dim = x.shape
    cols = w.shape[1]
    vmem = pl.BlockSpec(memory_space=pltpu.VMEM)
    hbm = pl.BlockSpec(memory_space=pl.ANY)
    return pl.pallas_call(
        functools.partial(gather_kernel, n),
        out_shape=(
            jax.ShapeDtypeStruct((n, rows, dim), BF16),
            jax.ShapeDtypeStruct((n, rows, cols), F32),
            jax.ShapeDtypeStruct((n, 1, rows), F32),
        ),
        in_specs=[vmem, vmem, vmem, hbm],
        out_specs=(hbm, hbm, vmem),
        scratch_shapes=[
            pltpu.VMEM((dim, cols), BF16),
            pltpu.VMEM((n, rows, dim), BF16),
            pltpu.VMEM((2, rows, cols), F32),
            pltpu.VMEM((rows // 2, 128), F32),
            pltpu.SemaphoreType.DMA,
            pltpu.SemaphoreType.DMA((2,)),
            pltpu.SemaphoreType.DMA((2,)),
            pltpu.SemaphoreType.DMA((4, 2, 2)),
            pltpu.SemaphoreType.DMA((4, 2, 2)),
            pltpu.SemaphoreType.DMA((n, 2, 2)),
            pltpu.SemaphoreType.DMA((n, 2, 2)),
        ],
        compiler_params=pltpu.CompilerParams(collective_id=0, has_side_effects=True, vmem_limit_bytes=VMEM_LIMIT),
        name="gather_logits",
    )(x, gain.reshape(1, dim), bias.reshape(1, dim), w)


def greet_all(n, me):
    barrier = pltpu.get_barrier_semaphore()
    for d in range(1, n):
        pl.semaphore_signal(barrier, inc=1, device_id={"vp": lax.rem(me + d, n)}, device_id_type=MESH)
    pl.semaphore_wait(barrier, n - 1)


def stats_kernel(n, mine_ref, tok_ref, lse_ref, toks_ref, got, total, send_a, recv_a, send_b, recv_b, send_c, recv_c):
    me = lax.axis_index("vp")
    greet_all(n, me)

    def hop(src, dst, send_sem, recv_sem, d):
        return pltpu.make_async_remote_copy(
            src_ref=src, dst_ref=dst, send_sem=send_sem.at[d], recv_sem=recv_sem.at[d],
            device_id={"vp": lax.rem(me + d, n)}, device_id_type=MESH)

    def first(d):
        return hop(mine_ref.at[lax.rem(me + d, n)], got.at[d], send_a, recv_a, d)

    def toks(d):
        return hop(tok_ref, toks_ref.at[me], send_b, recv_b, d)

    def second(d):
        return hop(total, lse_ref.at[me], send_c, recv_c, d)

    @pl.loop(1, n)
    def _(d):
        first(d).start()

    @pl.loop(1, n)
    def _(d):
        toks(d).start()

    got[0] = mine_ref[me]
    toks_ref[me] = tok_ref[...]

    @pl.loop(1, n)
    def _(d):
        first(d).wait_recv()

    parts = got[...]
    top = jnp.max(parts, axis=0)
    lse = top + jnp.log(jnp.sum(jnp.exp(parts - top[None]), axis=0))
    total[...] = lse
    lse_ref[me] = lse

    @pl.loop(1, n)
    def _(d):
        second(d).start()

    @pl.loop(1, n)
    def _(d):
        second(d).wait()
        toks(d).wait()
        first(d).wait_send()


def token_stats(n, mine, toks):
    rows = mine.shape[-1]
    vmem = pl.BlockSpec(memory_space=pltpu.VMEM)
    return pl.pallas_call(
        functools.partial(stats_kernel, n),
        out_shape=(jax.ShapeDtypeStruct((n, 1, rows), F32), jax.ShapeDtypeStruct((n, 1, 2 * rows), F32)),
        in_specs=[vmem, vmem],
        out_specs=(vmem, vmem),
        scratch_shapes=[pltpu.VMEM((n, 1, rows), F32), pltpu.VMEM((1, rows), F32)]
        + [pltpu.SemaphoreType.DMA((n,))] * 6,
        compiler_params=pltpu.CompilerParams(collective_id=1, has_side_effects=True),
        name="token_stats",
    )(mine, toks)


SLOTS = 8
LAG = 2
PIECES = 4


def scatter_kernel(n, z_hbm, h_hbm, w_hbm, lse_ref, toks_ref, dw_hbm, dh_ref, t_ref,
                   w_v, dw, zb, hb, dzb, part, from_x, from_s, flat, cols, total, w_sem, z_sem, h_sem, dw_sem,
                   send_x, send_s, recv_x, recv_s, credit_x, credit_s):
    ring = Rings(n)
    rows, dim = dh_ref.shape
    vocab = w_v.shape[1]
    half, quart, wide = rows // 2, rows // 4, dim // PIECES
    xo = pl.multiple_of(half * ring.core, half)
    so = pl.multiple_of(half * (1 - ring.core), half)
    col_start = ring.me * vocab

    w_copy = pltpu.make_async_copy(w_hbm, w_v, w_sem)
    w_copy.start()
    ring.greet()

    def fetch(hbm, buf, sem, j):
        slot = lax.rem(j, 2)
        return [
            pltpu.make_async_copy(
                hbm.at[lax.rem(j + ahead, n), pl.ds(off, half)], buf.at[slot, pl.ds(off, half)], sem.at[slot, ahead])
            for ahead, off in ((0, xo), (1, so))
        ]

    for copy in fetch(z_hbm, zb, z_sem, 0) + fetch(h_hbm, hb, h_sem, 0) + fetch(z_hbm, zb, z_sem, 1):
        copy.start()

    mask_total = jnp.sum(jnp.sum(toks_ref[:, :, rows:], axis=0), axis=-1, keepdims=True)
    total[...] = jnp.zeros_like(total)
    flat[...] = jnp.zeros_like(flat)
    t_ref[...] = jnp.zeros_like(t_ref)
    dw[...] = jnp.zeros_like(dw)

    def columns(j):
        for q in range(4):
            is_x = ring.core == q // 2
            group = lax.rem(jnp.where(is_x, j, j + 1), n)
            valid = jnp.where(is_x, jnp.where((j >= 1) & (j <= n), 1.0, 0.0), jnp.where(j < n, 1.0, 0.0))
            who = ring.owner(group, q)
            lanes = slice(q * quart, (q + 1) * quart)
            flat[0:1, lanes] = toks_ref[who][:, lanes] - col_start.astype(F32)
            flat[1:2, lanes] = toks_ref[who][:, rows + q * quart:rows + (q + 1) * quart] * valid / mask_total
            flat[2:3, lanes] = lse_ref[who][:, lanes]
        cols[...] = jnp.transpose(flat[...])

    dz_rows = min(16, quart)

    def make_dz(j, u):
        slot = lax.rem(j, 2)
        for b in range(rows // PIECES // dz_rows):
            r = pl.ds(u * (rows // PIECES) + b * dz_rows, dz_rows)
            z = zb[slot, r, :]
            label = cols[r, 0:1].astype(jnp.int32)
            weight = cols[r, 1:2]
            prob = jnp.exp(z - cols[r, 2:3])
            hit = lax.broadcasted_iota(jnp.int32, z.shape, 1) == label
            dzb[slot, r, :] = (jnp.where(hit, prob - 1.0, prob) * weight).astype(BF16)
            taken = jnp.where(hit, z * weight, 0.0)
            acc = taken[:, 0:128]
            for v in range(1, vocab // 128):
                acc = acc + taken[:, v * 128:(v + 1) * 128]
            t_ref[...] += acc

    def matmuls(j, u, slot):
        dz = dzb[lax.rem(j, 2)]
        d = slice(u * wide, (u + 1) * wide)
        part[slot] = lax.dot_general(dz, w_v[d, :], (((1,), (1,)), ((), ())), preferred_element_type=F32)
        dw[d, :] += lax.dot_general(hb[lax.rem(j, 2), :, d], dz, (((0,), (0,)), ((), ())), preferred_element_type=F32)

    def x_copy(k, c):
        slot = lax.rem(k, SLOTS)
        return pltpu.make_async_remote_copy(
            src_ref=part.at[slot, pl.ds(xo + c * quart, quart)], dst_ref=from_s.at[slot, c],
            send_sem=send_x.at[slot, c], recv_sem=recv_s.at[slot, c],
            device_id={"vp": ring.sibling}, device_id_type=MESH)

    def s_copy(k, c):
        slot = lax.rem(k, SLOTS)
        return pltpu.make_async_remote_copy(
            src_ref=part.at[slot, pl.ds(so + c * quart, quart)], dst_ref=from_x.at[slot, c],
            send_sem=send_s.at[slot, c], recv_sem=recv_x.at[slot, c],
            device_id={"vp": ring.s_next[c]}, device_id_type=MESH)

    def x_arrived(k, c):
        s_copy(k, c).wait_recv()

    def s_arrived(k, c):
        x_copy(k, c).wait_recv()

    x_lo, x_hi = PIECES, PIECES * n
    s_hi = PIECES * (n - 1)

    def do_x(j, u, k, slot):
        @pl.when(k >= SLOTS)
        def _():
            for c in range(2):
                x_arrived(k, c)
                r = pl.ds(xo + c * quart, quart)
                part[slot, r, :] += from_x[slot, c]

                @pl.when(k < s_hi)
                def _():
                    pl.semaphore_signal(credit_s.at[c], inc=1, device_id={"vp": ring.x_prev[c]}, device_id_type=MESH)

        @pl.when((k >= x_lo) & (k < x_hi))
        def _():
            for c in range(2):
                @pl.when(k >= x_lo + SLOTS)
                def _():
                    pl.semaphore_wait(credit_x.at[c], 1)
                x_copy(k, c).start()

        @pl.when(j == n)
        def _():
            dh_ref[pl.ds(xo, half), u * wide:(u + 1) * wide] = part[slot, pl.ds(xo, half), :]

    def do_s(j, u, k, slot):
        @pl.when((k >= x_lo) & (k < x_hi))
        def _():
            for c in range(2):
                s_arrived(k, c)
                r = pl.ds(so + c * quart, quart)
                part[slot, r, :] += from_s[slot, c]

                @pl.when(k < x_hi - SLOTS)
                def _():
                    pl.semaphore_signal(credit_x.at[c], inc=1, device_id={"vp": ring.sibling}, device_id_type=MESH)

        @pl.when((k >= 0) & (k < s_hi))
        def _():
            for c in range(2):
                @pl.when(k >= SLOTS)
                def _():
                    pl.semaphore_wait(credit_s.at[c], 1)
                s_copy(k, c).start()

        @pl.when(j == n - 1)
        def _():
            dh_ref[pl.ds(so, half), u * wide:(u + 1) * wide] = part[slot, pl.ds(so, half), :]

    for copy in fetch(z_hbm, zb, z_sem, 0):
        copy.wait()
    columns(0)
    for u in range(PIECES):
        make_dz(0, u)
    for copy in fetch(h_hbm, hb, h_sem, 0):
        copy.wait()
    w_copy.wait()
    ring.greeted()

    @pl.loop(0, n + 1)
    def _(j):
        @pl.when(j < n)
        def _():
            for copy in fetch(z_hbm, zb, z_sem, j + 1):
                copy.wait()
            for copy in fetch(h_hbm, hb, h_sem, j + 1):
                copy.start()

        @pl.when(j < n - 1)
        def _():
            for copy in fetch(z_hbm, zb, z_sem, j + 2):
                copy.start()

        columns(j + 1)
        for u in range(PIECES):
            k = PIECES * j + u
            slot = lax.rem(k, SLOTS)

            @pl.when((k >= SLOTS + x_lo))
            def _():
                for c in range(2):
                    x_copy(k - SLOTS, c).wait_send()

            @pl.when((k >= SLOTS) & (k < s_hi + SLOTS))
            def _():
                for c in range(2):
                    s_copy(k - SLOTS, c).wait_send()

            matmuls(j, u, slot)
            make_dz(j + 1, u)
            do_x(j, u, k, slot)
            ks = k - LAG
            js = j if u >= LAG else j - 1
            do_s(js, (u - LAG) % PIECES, ks, lax.rem(ks + SLOTS, SLOTS))

        @pl.when(j < n)
        def _():
            for copy in fetch(h_hbm, hb, h_sem, j + 1):
                copy.wait()

    dw_out = pltpu.make_async_copy(dw, dw_hbm, dw_sem)
    dw_out.start()
    for u in range(PIECES):
        for c in range(2):
            x_copy(x_hi - PIECES + u, c).wait_send()
    dw_out.wait()


def scatter_grads(n, z, h, w, lse, toks):
    _, rows, vocab = z.shape
    dim = w.shape[0]
    vmem = pl.BlockSpec(memory_space=pltpu.VMEM)
    hbm = pl.BlockSpec(memory_space=pl.ANY)
    wide = dim // PIECES
    return pl.pallas_call(
        functools.partial(scatter_kernel, n),
        out_shape=(
            jax.ShapeDtypeStruct((dim, vocab), F32),
            jax.ShapeDtypeStruct((rows, dim), F32),
            jax.ShapeDtypeStruct((16, 128), F32),
        ),
        in_specs=[hbm, hbm, hbm, vmem, vmem],
        out_specs=(hbm, vmem, vmem),
        scratch_shapes=[
            pltpu.VMEM((dim, vocab), BF16),
            pltpu.VMEM((dim, vocab), F32),
            pltpu.VMEM((2, rows, vocab), F32),
            pltpu.VMEM((2, rows, dim), BF16),
            pltpu.VMEM((2, rows, vocab), BF16),
            pltpu.VMEM((SLOTS, rows, wide), F32),
            pltpu.VMEM((SLOTS, 2, rows // 4, wide), F32),
            pltpu.VMEM((SLOTS, 2, rows // 4, wide), F32),
            pltpu.VMEM((128, rows), F32),
            pltpu.VMEM((rows, 128), F32),
            pltpu.VMEM((8, 128), F32),
            pltpu.SemaphoreType.DMA,
            pltpu.SemaphoreType.DMA((2, 2)),
            pltpu.SemaphoreType.DMA((2, 2)),
            pltpu.SemaphoreType.DMA,
            pltpu.SemaphoreType.DMA((SLOTS, 2)),
            pltpu.SemaphoreType.DMA((SLOTS, 2)),
            pltpu.SemaphoreType.DMA((SLOTS, 2)),
            pltpu.SemaphoreType.DMA((SLOTS, 2)),
            pltpu.SemaphoreType.REGULAR((2,)),
            pltpu.SemaphoreType.REGULAR((2,)),
        ],
        compiler_params=pltpu.CompilerParams(collective_id=2, has_side_effects=True, vmem_limit_bytes=VMEM_LIMIT),
        name="scatter_grads",
    )(z, h, w, lse, toks)


def finish_kernel(n, dh_ref, x_ref, gain_ref, t_ref, lse_ref, toks_ref, dx_ref, sums_ref, loss_ref, mine, got, send_sem, recv_sem):
    me = lax.axis_index("vp")
    rows, dim = dh_ref.shape
    blk = min(16, rows)
    barrier = pltpu.get_barrier_semaphore()
    for d in range(1, n):
        pl.semaphore_signal(barrier, inc=1, device_id={"vp": lax.rem(me + d, n)}, device_id_type=MESH)

    def body(b, carry):
        dg, dc = carry
        r = pl.ds(pl.multiple_of(b * blk, blk), blk)
        normed, inv_std = norm_rows(x_ref[r, :])
        dh = dh_ref[r, :]
        dg = dg + jnp.sum(dh * normed, axis=0, keepdims=True)
        dc = dc + jnp.sum(dh, axis=0, keepdims=True)
        scaled = dh * (1.0 + gain_ref[...])
        mean_s = jnp.mean(scaled, axis=-1, keepdims=True)
        mean_sn = jnp.mean(scaled * normed, axis=-1, keepdims=True)
        dx_ref[r, :] = (inv_std * (scaled - mean_s - normed * mean_sn)).astype(BF16)
        return dg, dc

    zero = jnp.zeros((1, dim), F32)
    dg, dc = lax.fori_loop(0, rows // blk, body, (zero, zero))
    mine[:, 0:dim] = dg
    mine[:, dim:2 * dim] = dc
    mine[:, 2 * dim:] = jnp.sum(t_ref[...], axis=0, keepdims=True)
    pl.semaphore_wait(barrier, n - 1)

    def hop(d):
        return pltpu.make_async_remote_copy(
            src_ref=mine, dst_ref=got.at[me], send_sem=send_sem.at[d], recv_sem=recv_sem.at[d],
            device_id={"vp": lax.rem(me + d, n)}, device_id_type=MESH)

    @pl.loop(1, n)
    def _(d):
        hop(d).start()

    got[me] = mine[...]
    mask = toks_ref[:, :, rows:]
    mask_total = jnp.sum(jnp.sum(mask, axis=0), axis=-1, keepdims=True)
    lse_sum = jnp.sum(jnp.sum(lse_ref[...] * (mask / mask_total[None]), axis=0), axis=-1, keepdims=True)

    @pl.loop(1, n)
    def _(d):
        hop(d).wait()

    sums = jnp.sum(got[...], axis=0)
    sums_ref[...] = sums[:, :2 * dim]
    loss_ref[...] = jnp.broadcast_to(lse_sum - jnp.sum(sums[:, 2 * dim:], axis=-1, keepdims=True), loss_ref.shape)


def finish(n, dh, x, gain, t, lse, toks):
    rows, dim = dh.shape
    vmem = pl.BlockSpec(memory_space=pltpu.VMEM)
    return pl.pallas_call(
        functools.partial(finish_kernel, n),
        out_shape=(
            jax.ShapeDtypeStruct((rows, dim), BF16),
            jax.ShapeDtypeStruct((1, 2 * dim), F32),
            jax.ShapeDtypeStruct((1, 128), F32),
        ),
        in_specs=[vmem] * 6,
        out_specs=(vmem, vmem, vmem),
        scratch_shapes=[
            pltpu.VMEM((1, 2 * dim + 128), F32),
            pltpu.VMEM((n, 1, 2 * dim + 128), F32),
            pltpu.SemaphoreType.DMA((n,)),
            pltpu.SemaphoreType.DMA((n,)),
        ],
        compiler_params=pltpu.CompilerParams(collective_id=3, has_side_effects=True),
        name="finish",
    )(dh, x, gain.reshape(1, dim), t, lse, toks)


def solution(mesh):
    n = mesh.shape["vp"]

    def per_device(hidden, norm_gain, norm_bias, w_blk, labels, loss_mask):
        dim = hidden.shape[-1]
        x = hidden.reshape(-1, dim)
        rows = x.shape[0]
        h, z, mine = gather_logits(n, x, norm_gain, norm_bias, w_blk)
        toks_mine = jnp.concatenate([labels.reshape(1, rows).astype(F32), loss_mask.reshape(1, rows)], axis=1)
        lse, toks = token_stats(n, mine, toks_mine)
        grad_w, dh, t = scatter_grads(n, z, h, w_blk, lse, toks)
        grad_x, sums, loss = finish(n, dh, x, norm_gain, t, lse, toks)
        return loss[0, :1], grad_x.reshape(hidden.shape), grad_w, sums[0, :dim], sums[0, dim:]

    tok_spec = P("vp", "dp")
    return jax.shard_map(
        per_device,
        mesh=mesh,
        in_specs=(P("vp", "dp", None), P(None), P(None), P(None, "vp"), tok_spec, tok_spec),
        out_specs=(P("dp"), P("vp", "dp", None), P("dp", "vp"), P("dp"), P("dp")),
        check_vma=False,
    )
```

time: 711 us -> 356 us (0.50)
  Pallas kernels: 0 us -> 337 us
  waiting for transfers between devices: 255 us -> 0 us
  blocking collectives: 202 us -> 0 us
  matrix products: 200 us -> 0 us
  other arithmetic: 32.8 us -> 1.27 us
  between operations: 16.7 us -> 2.42 us
  local copies, waits for them, and re-layouts: 2.32 us -> 15.1 us
    pallas_call x0 -> x4, Pallas kernels: none -> 337 us  [the longest x1 195 us: scatter_grads(): pl.pallas_call(functools.partial(scatter_kernel, n), out_shape=(jax.Shape...]
    reduce_scatter x1 -> x0, waiting for transfers between devices: 209 us -> none  [per_device(): lax.psum_scatter(grad_h_part, 'vp', scatter_dimension=0, tiled=True)]
    dot_general x3 -> x0, matrix products: 200 us -> none  [the longest x1 73.5 us: per_device(): jnp.einsum('sbd,sbv->dv', h_all, grad_logits, preferred_element_type=jnp....]
    psum x2 -> x0, blocking collectives: 90.5 us -> none  [the longest x1 45.7 us: per_device(): target = lax.psum(jnp.sum(jnp.where(is_label, logits, 0.0), axis=-1), 'vp')]
    all_gather x2 -> x0, blocking collectives: 66.9 us -> none  [the longest x1 33.5 us: per_device(): mask_all = lax.all_gather(loss_mask, 'vp', axis=0, tiled=True)]
    all_gather x1 -> x0, waiting for transfers between devices: 45.9 us -> none  [per_device(): h_all = lax.all_gather(h_bf, 'vp', axis=0, tiled=True)]
    pmax x1 -> x0, blocking collectives: 44.8 us -> none  [per_device(): row_max = lax.pmax(jnp.max(logits, axis=-1), 'vp')]
    reduce_sum x6 -> x0, other arithmetic: 25.6 us -> none  [the longest x1 17.1 us: per_device(): sum_exp = lax.psum(jnp.sum(exp_shift, axis=-1), 'vp')]
  transfers between devices with their start and end apart: 2 -> 0, of which waited for: 2 -> 0; matrix products, arithmetic and copies ran while one was open for 11% -> 0% of each run, Pallas kernels for 0% -> 0%
where the time goes in v1:
time: 356 us; the launch traced here: 355 us
  Pallas kernels  337 us (95%)
  local copies, waits for them, and re-layouts  15.1 us (4%)
    pallas_call x1, Pallas kernels, scatter_grads(): pl.pallas_call(functools.partial(scatter_kernel, n), out_shape=(jax.Shape...  195 us
    pallas_call x1, Pallas kernels, gather_logits(): pl.pallas_call(functools.partial(gather_kernel, n), out_shape=(jax.ShapeD...  107 us
    pallas_call x1, Pallas kernels, finish(): pl.pallas_call(functools.partial(finish_kernel, n), out_shape=(jax.ShapeD...  18.5 us
    pallas_call x1, Pallas kernels, token_stats(): pl.pallas_call(functools.partial(stats_kernel, n), out_shape=(jax.ShapeDt...  15.5 us
    unnamed x2, local copies, waits for them, and re-layouts  12.9 us

profile of v1, /device:TPU:97, one launch (start us, length us, event | category | flops | bytes accessed | tf_op | source)
XLA Modules:
  0.0 355.4 jit_solution(991010428501867370)
XLA Ops:
  0.6 0.8 reshape.43
  1.4 0.7 convert_element_type.14
  2.1 0.1 convert_element_type.15
  2.2 0.6 pad_maximum_fusion.tok_ref
  2.8 107.2 %gather_logits.1 = (bf16[32,256,2048]{2,1,0:T(8,128)(2,1)}, f32[32,256,1536]{2,1,0:T(8,128)}, f32[32,1,256]{2,1,0:T(1,128)}) custom-call(bf16[256,2048]{1,0:T(8,128)(2,1)} %bitcast.8, f32[1,2048]{1,0:T(1,128)} %bitcast.11, f32[1,2048]{1,0:T(1,128)} %bitcast.13, bf16[2048,1536]{1,0:T(8,128)(2,1)} %w_hbm.3), custom_call_target="tpu_custom_call" | custom-call | tf_op jit(solution)/shard_map/gather_logits/pallas_call | solution.py:216
  110.0 15.5 %token_stats.1 = (f32[32,1,256]{2,1,0:T(1,128)}, f32[32,1,512]{2,1,0:T(1,128)}) custom-call(f32[32,1,256]{2,1,0:T(1,128)} %get-tuple-element.18.mine_ref, f32[1,512]{1,0:T(1,128)} %pad_maximum_fusion.tok_ref), custom_call_target="tpu_custom_call" | custom-call | tf_op jit(solution)/shard_map/token_stats/pallas_call | solution.py:303
  125.5 195.4 %scatter_grads.1 = (f32[2048,1536]{1,0:T(8,128)}, f32[256,2048]{1,0:T(8,128)}, f32[16,128]{1,0:T(8,128)}) custom-call(f32[32,256,1536]{2,1,0:T(8,128)} %get-tuple-element.16.z_hbm, bf16[32,256,2048]{2,1,0:T(8,128)(2,1)} %get-tuple-element.17.h_hbm, bf16[2048,1536]{1,0:T(8,128)(2,1)} %w_hbm.3, f32[32,1,256]{2,1,0:T(1,128)} %get-tuple-element.19.lse_ref, ...), custom_call_target="tpu_custom_call" | custom-call | tf_op jit(solution)/shard_map/scatter_grads/pallas_call | solution.py:524
  320.9 18.5 %finish.1 = (bf16[256,2048]{1,0:T(8,128)(2,1)}, f32[1,4096]{1,0:T(1,128)}, f32[1,128]{1,0:T(1,128)}) custom-call(f32[256,2048]{1,0:T(8,128)} %get-tuple-element.21.dh_ref, bf16[256,2048]{1,0:T(8,128)(2,1)} %bitcast.9, f32[1,2048]{1,0:T(1,128)} %bitcast.12, f32[16,128]{1,0:T(8,128)} %get-tuple-element.22.t_ref, f32[32,1,256]{2,1,0:T(1,128)} %get-tuple-element.19.lse_ref, ...), custom_call_target="tpu_custom_call" | custom-call | tf_op jit(solution)/shard_map/finish/pallas_call | solution.py:615
  339.4 1.3 fusion
  341.3 2.3 copy.15
  343.6 10.6 %copy.16 = f32[2048,1536]{1,0:T(8,128)} copy(f32[2048,1536]{1,0:T(8,128)} %get-tuple-element.36) | data formatting | bytes 25165824

commit v2 on v0

v2 whole, which is shorter than its diff:
```python
import functools
import math

import jax
import jax.numpy as jnp
from jax import lax
from jax.experimental import pallas as pl
from jax.experimental.pallas import tpu as pltpu
from jax.sharding import PartitionSpec as P

NORM_EPS = 1e-5
MESH = pl.DeviceIdType.MESH
GATHER_VMEM = 62_000_000
F32 = jnp.float32
BF16 = jnp.bfloat16


class Rings:
    def __init__(self, n):
        self.n = n
        self.chips = n // 2
        self.side = math.isqrt(self.chips)
        assert self.side * self.side * 2 == n
        self.me = lax.axis_index("vp")
        self.core = lax.rem(self.me, 2)
        chip = lax.div(self.me, 2)
        x, y = lax.rem(chip, self.side), lax.div(chip, self.side)
        k = lax.rem(x + y, self.side)
        self.spot = (y * self.side + k, x * self.side + k)
        self.sibling = self.me + 1 - 2 * self.core
        step = 2 * self.core - 1
        self.s_next = [self.at(c, lax.rem(self.spot[c] + step + self.chips, self.chips), 1 - self.core) for c in range(2)]
        self.x_prev = [self.at(c, lax.rem(self.spot[c] + step + self.chips, self.chips), 1 - self.core) for c in range(2)]

    def at(self, cycle, spot, core):
        q, k = lax.div(spot, self.side), lax.rem(spot, self.side)
        a = lax.rem(k - q + self.side, self.side)
        chip = q * self.side + a if cycle == 0 else a * self.side + q
        return chip * 2 + core

    def owner(self, group, quarter):
        cycle = quarter % 2
        pos = 2 * self.spot[cycle] + self.core
        shift = self.n - group if quarter < 2 else group
        origin = lax.rem(pos + shift + self.n, self.n)
        return self.at(cycle, lax.div(origin, 2), lax.rem(origin, 2))

    def greet(self):
        barrier = pltpu.get_barrier_semaphore()
        for other in (self.sibling, *self.s_next):
            pl.semaphore_signal(barrier, inc=1, device_id={"vp": other}, device_id_type=MESH)

    def greeted(self):
        pl.semaphore_wait(pltpu.get_barrier_semaphore(), 3)


def norm_rows(x_rows):
    x = x_rows.astype(F32)
    centered = x - jnp.mean(x, axis=-1, keepdims=True)
    inv_std = lax.rsqrt(jnp.mean(centered * centered, axis=-1, keepdims=True) + NORM_EPS)
    return centered * inv_std, inv_std


def signal_all(n, me):
    barrier = pltpu.get_barrier_semaphore()
    for d in range(1, n):
        pl.semaphore_signal(barrier, inc=1, device_id={"vp": lax.rem(me + d, n)}, device_id_type=MESH)


def gather_kernel(n, x_ref, gain_ref, bias_ref, tok_ref, w_hbm, h_hbm, z_hbm, wt_hbm, lse_ref, toks_ref,
                  w_v, wt_v, h_all, zbuf, col, local, got, own, w_sem, wt_sem, h_sem, z_sem, send_x, send_s, send_d, recv_x, recv_s,
                  stat_send, stat_recv, lse_send, lse_recv, tok_send, tok_recv):
    ring = Rings(n)
    me = ring.me
    rows, dim = x_ref.shape
    cols = w_v.shape[1]
    half, quart, piece, wide = rows // 2, rows // 4, rows // 8, cols // 2
    xo = pl.multiple_of(half * ring.core, half)
    so = pl.multiple_of(half * (1 - ring.core), half)

    w_copy = pltpu.make_async_copy(w_hbm, w_v, w_sem)
    w_copy.start()
    signal_all(n, me)

    ln_rows = min(64, rows)

    @pl.loop(0, rows // ln_rows)
    def _(b):
        r = pl.ds(pl.multiple_of(b * ln_rows, ln_rows), ln_rows)
        normed, _ = norm_rows(x_ref[r, :])
        h_all[0, r, :] = (normed * (1.0 + gain_ref[...]) + bias_ref[...]).astype(BF16)

    pl.semaphore_wait(pltpu.get_barrier_semaphore(), n - 1)

    def hop(src, dst, send_sem, recv_sem, who):
        return pltpu.make_async_remote_copy(
            src_ref=src, dst_ref=dst, send_sem=send_sem, recv_sem=recv_sem,
            device_id={"vp": who}, device_id_type=MESH)

    def x_copy(i, c, u):
        r = pl.ds(xo + (c * quart + u * piece), piece)
        return hop(h_all.at[i, r], h_all.at[i + 1, r], send_x.at[lax.rem(i, 4), c, u], recv_s.at[i + 1, c, u], ring.sibling)

    def s_copy(i, c, u):
        r = pl.ds(so + (c * quart + u * piece), piece)
        return hop(h_all.at[i, r], h_all.at[i + 1, r], send_s.at[lax.rem(i, 4), c, u], recv_x.at[i + 1, c, u], ring.s_next[c])

    def d_copy(c, u):
        r = pl.ds(so + (c * quart + u * piece), piece)
        return hop(h_all.at[0, r], h_all.at[n - 1, r], send_d.at[c, u], recv_x.at[n - 1, c, u], ring.sibling)

    def x_arrived(i, c, u):
        r = pl.ds(xo + (c * quart + u * piece), piece)
        hop(h_all.at[i, r], h_all.at[i, r], send_s.at[0, c, u], recv_x.at[i, c, u], ring.s_next[c]).wait_recv()

    def s_arrived(i, c, u):
        r = pl.ds(so + (c * quart + u * piece), piece)
        hop(h_all.at[i, r], h_all.at[i, r], send_x.at[0, c, u], recv_s.at[i, c, u], ring.sibling).wait_recv()

    def send(copy, i, c, u):
        @pl.when(i >= 4)
        def _():
            copy(i - 4, c, u).wait_send()
        copy(i, c, u).start()

    def z_out(g, slot):
        return pltpu.make_async_copy(zbuf.at[slot], z_hbm.at[g], z_sem.at[slot])

    def h_out(g, slot):
        return pltpu.make_async_copy(h_all.at[g], h_hbm.at[g], h_sem.at[slot])

    stat_rows = min(32, half)

    def stats(slot, u):
        for b in range(half // stat_rows):
            z = zbuf[slot, u * half + b * stat_rows:u * half + (b + 1) * stat_rows, :]
            top = jnp.max(z, axis=-1, keepdims=True)
            lse = top + jnp.log(jnp.sum(jnp.exp(z - top), axis=-1, keepdims=True))
            col[b * stat_rows:(b + 1) * stat_rows, :] = jnp.broadcast_to(lse, (stat_rows, col.shape[1]))
        return jnp.transpose(col[...])[0:1, :]

    def stat_copy(g, u, c):
        q = 2 * u + c
        return hop(local.at[g, u], got.at[g, q], stat_send, stat_recv, ring.owner(g, q))

    def send_stats(g):
        for u in range(2):
            for c in range(2):
                stat_copy(g, u, c).start()

    def logits(g, slot, u):
        part = slice(u * wide, (u + 1) * wide)
        zbuf[slot, :, part] = jnp.dot(h_all[g], w_v[:, part], preferred_element_type=F32)

    strip = dim // n

    def flip(a, b):
        r = pl.ds(pl.multiple_of(a * (2 * strip), 2 * strip), 2 * strip)
        part = slice(b * wide, (b + 1) * wide)
        wt_v[part, r] = jnp.transpose(w_v[r, part])

    def tok_copy(d):
        return hop(tok_ref, toks_ref.at[me], tok_send, tok_recv, lax.rem(me + d, n))

    def lse_copy(d):
        return hop(own, lse_ref.at[me], lse_send, lse_recv, lax.rem(me + d, n))

    for c in range(2):
        s_copy(0, c, 0).start()
    zbuf[...] = jnp.zeros_like(zbuf)
    w_copy.wait()

    @pl.loop(0, n // 2)
    def _(a):
        for b in range(2):
            i = 2 * a + b
            for u in range(2):
                @pl.when(i >= 1)
                def _():
                    for c in range(2):
                        x_arrived(i, c, u)

                @pl.when(i < n - 1)
                def _():
                    for c in range(2):
                        send(x_copy, i, c, u)

                j = i + u

                @pl.when((j >= 1) & (j < n))
                def _():
                    for c in range(2):
                        s_arrived(j, c, 1 - u)

                @pl.when(j < n - 2)
                def _():
                    for c in range(2):
                        send(s_copy, j, c, 1 - u)

                if u == 0:
                    flip(a, b)
                else:
                    @pl.when(i == 0)
                    def _():
                        for c in range(2):
                            for v in range(2):
                                d_copy(c, v).start()

                        @pl.loop(1, n)
                        def _(d):
                            tok_copy(d).start()

                    @pl.when(i >= 3)
                    def _():
                        send_stats(i - 2)

                if u == 0:
                    @pl.when(i >= 1)
                    def _():
                        logits(i - 1, 1 - b, 1)
                        local[lax.max(i - 2, 0), 1] = stats(b, 1)
                        z_out(i - 1, 1 - b).start()
                else:
                    @pl.when(i >= 2)
                    def _():
                        z_out(i - 2, b).wait()
                        h_out(i - 2, b).wait()
                    h_out(i, b).start()
                    logits(i, b, 0)
                    local[lax.max(i - 1, 0), 0] = stats(1 - b, 0)

    last = n - 1
    wt_copy = pltpu.make_async_copy(wt_v, wt_hbm, wt_sem)
    wt_copy.start()
    logits(last, 1, 1)
    local[last - 1, 1] = stats(0, 1)
    z_out(last, 1).start()
    for u in range(2):
        local[last, u] = stats(1, u)
    send_stats(last - 1)
    send_stats(last)
    for q in range(4):
        got[0, q] = local[0, q // 2]
    toks_ref[me] = tok_ref[...]

    everyone = pl.ds(1, n - 1)
    stats_total = hop(got.at[everyone], got.at[everyone], stat_send, stat_recv, ring.sibling)
    stats_total.wait_recv()
    for q in range(4):
        parts = got[:, q]
        top = jnp.max(parts, axis=0)
        lse = top + jnp.log(jnp.sum(jnp.exp(parts - top[None]), axis=0))
        lanes = slice((q % 2) * quart, (q % 2 + 1) * quart)
        own[:, q * quart:(q + 1) * quart] = lse[:, lanes]
    lse_ref[me] = own[...]

    @pl.loop(1, n)
    def _(d):
        lse_copy(d).start()

    for c in range(2):
        for u in range(2):
            d_copy(c, u).wait_send()
            for i in range(n - 5, n - 1):
                x_copy(i, c, u).wait_send()
            for i in range(n - 6, n - 2):
                s_copy(i, c, u).wait_send()
    stats_total.wait_send()
    toks_total = hop(toks_ref.at[everyone], toks_ref.at[everyone], tok_send, tok_recv, ring.sibling)
    toks_total.wait_recv()
    toks_total.wait_send()
    wt_copy.wait()
    for g in (last - 1, last):
        z_out(g, g % 2).wait()
        h_out(g, g % 2).wait()
    lse_total = hop(lse_ref.at[everyone], lse_ref.at[everyone], lse_send, lse_recv, ring.sibling)
    lse_total.wait_recv()
    lse_total.wait_send()


def gather_logits(n, x, gain, bias, toks, w):
    rows, dim = x.shape
    cols = w.shape[1]
    vmem = pl.BlockSpec(memory_space=pltpu.VMEM)
    hbm = pl.BlockSpec(memory_space=pltpu.HBM)
    dma = pltpu.SemaphoreType.DMA
    return pl.pallas_call(
        functools.partial(gather_kernel, n),
        out_shape=(
            jax.ShapeDtypeStruct((n, rows, dim), BF16),
            jax.ShapeDtypeStruct((n, rows, cols), F32),
            jax.ShapeDtypeStruct((cols, dim), BF16),
            jax.ShapeDtypeStruct((n, 1, rows), F32),
            jax.ShapeDtypeStruct((n, 1, 2 * rows), F32),
        ),
        in_specs=[vmem, vmem, vmem, vmem, hbm],
        out_specs=(hbm, hbm, hbm, vmem, vmem),
        scratch_shapes=[
            pltpu.VMEM((dim, cols), BF16),
            pltpu.VMEM((cols, dim), BF16),
            pltpu.VMEM((n, rows, dim), BF16),
            pltpu.VMEM((2, rows, cols), F32),
            pltpu.VMEM((rows // 2, 128), F32),
            pltpu.VMEM((n, 2, 1, rows // 2), F32),
            pltpu.VMEM((n, 4, 1, rows // 2), F32),
            pltpu.VMEM((1, rows), F32),
            dma, dma, dma((2,)), dma((2,)), dma((4, 2, 2)), dma((4, 2, 2)), dma((2, 2)), dma((n, 2, 2)), dma((n, 2, 2)),
            dma, dma, dma, dma, dma, dma,
        ],
        compiler_params=pltpu.CompilerParams(collective_id=0, has_side_effects=True, vmem_limit_bytes=GATHER_VMEM),
        name="gather_logits",
    )(x, gain.reshape(1, dim), bias.reshape(1, dim), toks, w)


SLOTS = 8
LAG = 2
PIECES = 4
SCATTER_VMEM = 36_000_000


def scatter_kernel(n, z_hbm, h_hbm, w_hbm, lse_ref, toks_ref, dw, dh_ref, t_ref,
                   w_v, zb, hb, dzb, part, from_x, from_s, from_d, flat, cols, w_sem, z_sem, h_sem,
                   send_x, send_s, send_d, recv_x, recv_s, recv_d, credit_x, credit_s):
    ring = Rings(n)
    rows, dim = dh_ref.shape
    vocab = w_v.shape[0]
    half, quart, wide = rows // 2, rows // 4, dim // PIECES
    xo = pl.multiple_of(half * ring.core, half)
    so = pl.multiple_of(half * (1 - ring.core), half)
    col_start = ring.me * vocab

    ring.greet()

    def fetch(hbm, buf, sem, j, slot):
        return [
            pltpu.make_async_copy(
                hbm.at[lax.rem(j + ahead, n), pl.ds(off, half)], buf.at[slot, pl.ds(off, half)], sem.at[slot, ahead])
            for ahead, off in ((0, xo), (1, so))
        ]

    w_copy = pltpu.make_async_copy(w_hbm, w_v, w_sem)
    for copy in fetch(z_hbm, zb, z_sem, 1, 0) + [w_copy] + fetch(h_hbm, hb, h_sem, 1, 0) + fetch(z_hbm, zb, z_sem, 2, 1):
        copy.start()

    mask_total = jnp.sum(jnp.sum(toks_ref[:, :, rows:], axis=0), axis=-1, keepdims=True)
    flat[...] = jnp.zeros_like(flat)
    t_ref[...] = jnp.zeros_like(t_ref)

    def columns(j):
        valid = jnp.where(j <= n, 1.0, 0.0)
        for q in range(4):
            group = lax.rem(jnp.where(ring.core == q // 2, j, j + 1), n)
            who = ring.owner(group, q)
            lanes = slice(q * quart, (q + 1) * quart)
            flat[0:1, lanes] = toks_ref[who][:, lanes] - col_start.astype(F32)
            flat[1:2, lanes] = toks_ref[who][:, rows + q * quart:rows + (q + 1) * quart] * valid / mask_total
            flat[2:3, lanes] = lse_ref[who][:, lanes]
        cols[...] = jnp.transpose(flat[...])

    dz_rows = min(16, quart)

    def make_dz(slot, u):
        for b in range(rows // PIECES // dz_rows):
            r = slice(u * (rows // PIECES) + b * dz_rows, u * (rows // PIECES) + (b + 1) * dz_rows)
            z = zb[slot, r, :]
            label = cols[r, 0:1].astype(jnp.int32)
            weight = cols[r, 1:2]
            prob = jnp.exp(z - cols[r, 2:3])
            hit = lax.broadcasted_iota(jnp.int32, z.shape, 1) == label
            dzb[slot, r, :] = (jnp.where(hit, prob - 1.0, prob) * weight).astype(BF16)
            taken = jnp.where(hit, z * weight, 0.0)
            acc = taken[:, 0:128]
            for v in range(1, vocab // 128):
                acc = acc + taken[:, v * 128:(v + 1) * 128]
            t_ref[...] += acc

    def matmuls(now, u, slot):
        dz = dzb[now]
        d = slice(u * wide, (u + 1) * wide)
        part[slot] = jnp.dot(dz, w_v[:, d], preferred_element_type=F32)
        dw[d, :] += lax.dot_general(hb[now, :, d], dz, (((0,), (0,)), ((), ())), preferred_element_type=F32)

    def hop(src, dst, send_sem, recv_sem, who):
        return pltpu.make_async_remote_copy(
            src_ref=src, dst_ref=dst, send_sem=send_sem, recv_sem=recv_sem,
            device_id={"vp": who}, device_id_type=MESH)

    def x_rows(c):
        return pl.ds(xo + c * quart, quart)

    def s_rows(c):
        return pl.ds(so + c * quart, quart)

    def x_copy(slot, c):
        return hop(part.at[slot, x_rows(c)], from_s.at[slot, c], send_x.at[slot, c], recv_s.at[slot, c], ring.sibling)

    def s_copy(slot, c):
        return hop(part.at[slot, s_rows(c)], from_x.at[slot, c], send_s.at[slot, c], recv_x.at[slot, c], ring.s_next[c])

    def d_copy(slot, u, c):
        return hop(part.at[slot, s_rows(c)], from_d.at[u, c], send_d.at[u, c], recv_d.at[u, c], ring.sibling)

    first, end = PIECES, PIECES * n

    def do_x(j, k, slot):
        @pl.when((k >= first + SLOTS) & (k < end))
        def _():
            for c in range(2):
                s_copy(slot, c).wait_recv()
                part[slot, x_rows(c), :] += from_x[slot, c]

        @pl.when((k >= first + SLOTS) & (k < end - PIECES))
        def _():
            for c in range(2):
                pl.semaphore_signal(credit_s.at[c], inc=1, device_id={"vp": ring.s_next[c]}, device_id_type=MESH)

        @pl.when(k < end)
        def _():
            for c in range(2):
                @pl.when(k >= first + SLOTS)
                def _():
                    pl.semaphore_wait(credit_x.at[c], 1)
                x_copy(slot, c).start()

    def do_s(k, slot, u):
        @pl.when((k >= first) & (k < end))
        def _():
            for c in range(2):
                x_copy(slot, c).wait_recv()
                part[slot, s_rows(c), :] += from_s[slot, c]

        @pl.when((k >= first) & (k < end - SLOTS))
        def _():
            for c in range(2):
                pl.semaphore_signal(credit_x.at[c], inc=1, device_id={"vp": ring.sibling}, device_id_type=MESH)

        @pl.when((k >= first) & (k < end - PIECES))
        def _():
            for c in range(2):
                @pl.when(k >= first + SLOTS)
                def _():
                    pl.semaphore_wait(credit_s.at[c], 1)
                s_copy(slot, c).start()

        @pl.when((k >= end - PIECES) & (k < end))
        def _():
            dh_ref[pl.ds(so, half), u * wide:(u + 1) * wide] = part[slot, pl.ds(so, half), :]

    dw[...] = jnp.zeros_like(dw)
    columns(1)
    for copy in fetch(z_hbm, zb, z_sem, 1, 0):
        copy.wait()
    for u in range(PIECES):
        make_dz(0, u)
    for copy in fetch(h_hbm, hb, h_sem, 1, 0):
        copy.wait()
    w_copy.wait()
    ring.greeted()

    @pl.loop(0, n // 2)
    def _(a):
        for b in range(2):
            j = 2 * a + b + 1
            now, then = b, 1 - b

            @pl.when(j < n)
            def _():
                for copy in fetch(z_hbm, zb, z_sem, j + 1, then):
                    copy.wait()
                for copy in fetch(h_hbm, hb, h_sem, j + 1, then):
                    copy.start()

            @pl.when(j < n - 1)
            def _():
                for copy in fetch(z_hbm, zb, z_sem, j + 2, now):
                    copy.start()

            columns(j + 1)
            for u in range(PIECES):
                k = PIECES * j + u
                slot = (PIECES * (b + 1) + u) % SLOTS

                @pl.when(k >= first + SLOTS)
                def _():
                    for c in range(2):
                        x_copy(slot, c).wait_send()
                        s_copy(slot, c).wait_send()

                matmuls(now, u, slot)
                make_dz(then, u)

                @pl.when(j == n)
                def _():
                    for c in range(2):
                        d_copy(slot, u, c).start()

                do_x(j, k, slot)
                do_s(k - LAG, (slot - LAG) % SLOTS, (u - LAG) % PIECES)

            @pl.when(j < n)
            def _():
                for copy in fetch(h_hbm, hb, h_sem, j + 1, then):
                    copy.wait()

    for u in range(PIECES):
        slot = (end + u) % SLOTS
        for c in range(2):
            d_copy(slot, u, c).wait_recv()
            s_copy(slot, c).wait_recv()
            dh_ref[x_rows(c), u * wide:(u + 1) * wide] = part[slot, x_rows(c), :] + from_d[u, c] + from_x[slot, c]
    for u in range(PIECES):
        for c in range(2):
            x_copy((end - PIECES + u) % SLOTS, c).wait_send()
            d_copy((end + u) % SLOTS, u, c).wait_send()


def scatter_grads(n, z, h, w, lse, toks):
    _, rows, vocab = z.shape
    dim = w.shape[1]
    vmem = pl.BlockSpec(memory_space=pltpu.VMEM)
    hbm = pl.BlockSpec(memory_space=pltpu.HBM)
    dma = pltpu.SemaphoreType.DMA
    wide = dim // PIECES
    return pl.pallas_call(
        functools.partial(scatter_kernel, n),
        out_shape=(
            pltpu.VMEM((dim, vocab), F32),
            pltpu.VMEM((rows, dim), F32),
            pltpu.VMEM((16, 128), F32),
        ),
        in_specs=[hbm, hbm, hbm, vmem, vmem],
        out_specs=(vmem, vmem, vmem),
        scratch_shapes=[
            pltpu.VMEM((vocab, dim), BF16),
            pltpu.VMEM((2, rows, vocab), F32),
            pltpu.VMEM((2, rows, dim), BF16),
            pltpu.VMEM((2, rows, vocab), BF16),
            pltpu.VMEM((SLOTS, rows, wide), F32),
            pltpu.VMEM((SLOTS, 2, rows // 4, wide), F32),
            pltpu.VMEM((SLOTS, 2, rows // 4, wide), F32),
            pltpu.VMEM((PIECES, 2, rows // 4, wide), F32),
            pltpu.VMEM((128, rows), F32),
            pltpu.VMEM((rows, 128), F32),
            dma, dma((2, 2)), dma((2, 2)),
            dma((SLOTS, 2)), dma((SLOTS, 2)), dma((PIECES, 2)), dma((SLOTS, 2)), dma((SLOTS, 2)), dma((PIECES, 2)),
            pltpu.SemaphoreType.REGULAR((2,)),
            pltpu.SemaphoreType.REGULAR((2,)),
        ],
        compiler_params=pltpu.CompilerParams(collective_id=1, has_side_effects=True, vmem_limit_bytes=SCATTER_VMEM),
        name="scatter_grads",
    )(z, h, w, lse, toks)


def local_kernel(dh_ref, x_ref, gain_ref, t_ref, dw_ref, dx_ref, sums_ref, dw_hbm, dw_sem):
    rows, dim = dh_ref.shape
    blk = min(64, rows)
    dw_copy = pltpu.make_async_copy(dw_ref, dw_hbm, dw_sem)
    dw_copy.start()

    def body(b, carry):
        dg, dc = carry
        r = pl.ds(pl.multiple_of(b * blk, blk), blk)
        normed, inv_std = norm_rows(x_ref[r, :])
        dh = dh_ref[r, :]
        dhn = dh * normed
        scaled = dh * (1.0 + gain_ref[...])
        mean_s = jnp.mean(scaled, axis=-1, keepdims=True)
        mean_sn = jnp.mean(scaled * normed, axis=-1, keepdims=True)
        dx_ref[r, :] = (inv_std * (scaled - mean_s - normed * mean_sn)).astype(BF16)
        return dg + jnp.sum(dhn, axis=0, keepdims=True), dc + jnp.sum(dh, axis=0, keepdims=True)

    zero = jnp.zeros((1, dim), F32)
    dg, dc = lax.fori_loop(0, rows // blk, body, (zero, zero))
    sums_ref[0, :, 0:dim] = dg
    sums_ref[1, :, 0:dim] = dc
    sums_ref[0, :, dim:] = jnp.sum(t_ref[...], axis=0, keepdims=True)
    sums_ref[1, :, dim:] = jnp.zeros((1, 128), F32)
    dw_copy.wait()


def local_backward(dh, x, gain, t, dw):
    rows, dim = dh.shape
    vmem = pl.BlockSpec(memory_space=pltpu.VMEM)
    return pl.pallas_call(
        local_kernel,
        out_shape=(
            jax.ShapeDtypeStruct((rows, dim), BF16),
            jax.ShapeDtypeStruct((2, 1, dim + 128), F32),
            jax.ShapeDtypeStruct(dw.shape, F32),
        ),
        in_specs=[vmem] * 5,
        out_specs=(vmem, vmem, pl.BlockSpec(memory_space=pltpu.HBM)),
        scratch_shapes=[pltpu.SemaphoreType.DMA],
        compiler_params=pltpu.CompilerParams(vmem_limit_bytes=24_000_000),
        name="local_backward",
    )(dh, x, gain.reshape(1, dim), t, dw)


def sums_kernel(n, mine_ref, lse_ref, toks_ref, dg_ref, dc_ref, loss_ref,
                near, both, chips, total, send_a, recv_a, send_b, recv_b, send_c, recv_c):
    me = lax.axis_index("vp")
    core, chip = lax.rem(me, 2), lax.div(me, 2)
    count = n // 2
    sibling = me + 1 - 2 * core
    dim = dg_ref.shape[1]
    rows = lse_ref.shape[-1]

    def peer(d):
        return 2 * lax.rem(chip + d, count) + core

    barrier = pltpu.get_barrier_semaphore()
    pl.semaphore_signal(barrier, inc=1, device_id={"vp": sibling}, device_id_type=MESH)
    for d in range(1, count):
        pl.semaphore_signal(barrier, inc=1, device_id={"vp": peer(d)}, device_id_type=MESH)

    mask = toks_ref[:, :, rows:]
    mask_total = jnp.sum(jnp.sum(mask, axis=0), axis=-1, keepdims=True)
    lse_sum = jnp.sum(jnp.sum(lse_ref[...] * (mask / mask_total[None]), axis=0), axis=-1, keepdims=True)
    pl.semaphore_wait(barrier, count)

    def hop(src, dst, send_sem, recv_sem, who):
        return pltpu.make_async_remote_copy(
            src_ref=src, dst_ref=dst, send_sem=send_sem, recv_sem=recv_sem,
            device_id={"vp": who}, device_id_type=MESH)

    first = hop(mine_ref, near, send_a, recv_a, sibling)
    first.start()
    first.wait_recv()
    both[...] = mine_ref[core] + near[core]

    def second(d):
        return hop(both, chips.at[chip], send_b.at[d], recv_b.at[d], peer(d))

    @pl.loop(1, count)
    def _(d):
        second(d).start()

    chips[chip] = both[...]

    @pl.loop(1, count)
    def _(d):
        second(d).wait()

    total[core] = jnp.sum(chips[...], axis=0)
    third = hop(total.at[core], total.at[core], send_c, recv_c, sibling)
    third.start()
    first.wait_send()
    third.wait()
    dg_ref[...] = total[0, :, 0:dim]
    dc_ref[...] = total[1, :, 0:dim]
    loss_ref[...] = lse_sum - jnp.sum(total[0, :, dim:], axis=-1, keepdims=True)


def group_sums(n, mine, lse, toks):
    wide = mine.shape[-1]
    dim = wide - 128
    vmem = pl.BlockSpec(memory_space=pltpu.VMEM)
    dma = pltpu.SemaphoreType.DMA
    return pl.pallas_call(
        functools.partial(sums_kernel, n),
        out_shape=(
            jax.ShapeDtypeStruct((1, dim), F32),
            jax.ShapeDtypeStruct((1, dim), F32),
            jax.ShapeDtypeStruct((1, 1), F32),
        ),
        in_specs=[vmem] * 3,
        out_specs=(vmem,) * 3,
        scratch_shapes=[
            pltpu.VMEM((2, 1, wide), F32),
            pltpu.VMEM((1, wide), F32),
            pltpu.VMEM((n // 2, 1, wide), F32),
            pltpu.VMEM((2, 1, wide), F32),
            dma, dma, dma((n // 2,)), dma((n // 2,)), dma, dma,
        ],
        compiler_params=pltpu.CompilerParams(collective_id=2, has_side_effects=True, vmem_limit_bytes=16_000_000),
        name="group_sums",
    )(mine, lse, toks)


def solution(mesh):
    n = mesh.shape["vp"]

    def per_device(hidden, norm_gain, norm_bias, w_blk, labels, loss_mask):
        dim = hidden.shape[-1]
        x = hidden.reshape(-1, dim)
        rows = x.shape[0]
        toks_mine = jnp.concatenate([labels.reshape(1, rows).astype(F32), loss_mask.reshape(1, rows)], axis=1)
        h, z, wt, lse, toks = gather_logits(n, x, norm_gain, norm_bias, toks_mine, w_blk)
        dw, dh, t = scatter_grads(n, z, h, wt, lse, toks)
        grad_x, sums, grad_w = local_backward(dh, x, norm_gain, t, dw)
        grad_gain, grad_bias, loss = group_sums(n, sums, lse, toks)
        return loss.reshape(1), grad_x.reshape(hidden.shape), grad_w, grad_gain.reshape(dim), grad_bias.reshape(dim)

    tok_spec = P("vp", "dp")
    return jax.shard_map(
        per_device,
        mesh=mesh,
        in_specs=(P("vp", "dp", None), P(None), P(None), P(None, "vp"), tok_spec, tok_spec),
        out_specs=(P("dp"), P("vp", "dp", None), P("dp", "vp"), P("dp"), P("dp")),
        check_vma=False,
    )
```

time: 711 us -> 322 us (0.45)
  Pallas kernels: 0 us -> 315 us
  waiting for transfers between devices: 255 us -> 0 us
  blocking collectives: 202 us -> 0 us
  matrix products: 200 us -> 0 us
  other arithmetic: 32.8 us -> 1.27 us
  between operations: 16.7 us -> 2.38 us
    pallas_call x0 -> x4, Pallas kernels: none -> 315 us  [the longest x1 182 us: scatter_grads(): pl.pallas_call(functools.partial(scatter_kernel, n), out_shape=(pltpu.VME...]
    reduce_scatter x1 -> x0, waiting for transfers between devices: 209 us -> none  [per_device(): lax.psum_scatter(grad_h_part, 'vp', scatter_dimension=0, tiled=True)]
    dot_general x3 -> x0, matrix products: 200 us -> none  [the longest x1 73.5 us: per_device(): jnp.einsum('sbd,sbv->dv', h_all, grad_logits, preferred_element_type=jnp....]
    psum x2 -> x0, blocking collectives: 90.5 us -> none  [the longest x1 45.7 us: per_device(): target = lax.psum(jnp.sum(jnp.where(is_label, logits, 0.0), axis=-1), 'vp')]
    all_gather x2 -> x0, blocking collectives: 66.9 us -> none  [the longest x1 33.5 us: per_device(): mask_all = lax.all_gather(loss_mask, 'vp', axis=0, tiled=True)]
    all_gather x1 -> x0, waiting for transfers between devices: 45.9 us -> none  [per_device(): h_all = lax.all_gather(h_bf, 'vp', axis=0, tiled=True)]
    pmax x1 -> x0, blocking collectives: 44.8 us -> none  [per_device(): row_max = lax.pmax(jnp.max(logits, axis=-1), 'vp')]
    reduce_sum x6 -> x0, other arithmetic: 25.6 us -> none  [the longest x1 17.1 us: per_device(): sum_exp = lax.psum(jnp.sum(exp_shift, axis=-1), 'vp')]
  transfers between devices with their start and end apart: 2 -> 0, of which waited for: 2 -> 0; matrix products, arithmetic and copies ran while one was open for 11% -> 0% of each run, Pallas kernels for 0% -> 0%
where the time goes in v2:
time: 322 us
  Pallas kernels  315 us (98%)
  local copies, waits for them, and re-layouts  3.64 us (1%)
    pallas_call x1, Pallas kernels, scatter_grads(): pl.pallas_call(functools.partial(scatter_kernel, n), out_shape=(pltpu.VME...  182 us
    pallas_call x1, Pallas kernels, gather_logits(): pl.pallas_call(functools.partial(gather_kernel, n), out_shape=(jax.ShapeD...  116 us
    pallas_call x1, Pallas kernels, group_sums(): pl.pallas_call(functools.partial(sums_kernel, n), out_shape=(jax.ShapeDty...  11.1 us

profile of v2, /device:TPU:97, one launch (start us, length us, event | category | flops | bytes accessed | tf_op | source)
XLA Modules:
  0.0 322.1 jit_solution(10177975431371143686)
XLA Ops:
  0.6 0.8 reshape.52
  1.4 0.7 convert_element_type.14
  2.1 0.1 convert_element_type.15
  2.2 0.6 pad_maximum_fusion.tok_ref
  2.8 115.8 %gather_logits.1 = (bf16[32,256,2048]{2,1,0:T(8,128)(2,1)}, f32[32,256,1536]{2,1,0:T(8,128)}, bf16[1536,2048]{1,0:T(8,128)(2,1)}, f32[32,1,256]{2,1,0:T(1,128)}, f32[32,1,512]{2,1,0:T(1,128)}) custom-call(bf16[256,2048]{1,0:T(8,128)(2,1)} %bitcast.7, f32[1,2048]{1,0:T(1,128)} %bitcast.9, f32[1,2048]{1,0:T(1,128)} %bitcast.13, ...), custom_call_target="tpu_custom_call" | custom-call | tf_op jit(solution)/shard_map/gather_logits/pallas_call | solution.py:287
  118.6 0.0 copy-start.1
  118.6 0.8 copy-done.1
  119.4 0.0 copy-start.2
  119.4 0.8 copy-done.2
  120.2 0.0 copy-start
  120.2 0.0 copy-start.3
  120.2 182.0 %scatter_grads.1 = (f32[2048,1536]{1,0:T(8,128)S(1)}, f32[256,2048]{1,0:T(8,128)S(1)}, f32[16,128]{1,0:T(8,128)S(1)}) custom-call(f32[32,256,1536]{2,1,0:T(8,128)} %get-tuple-element.19.z_hbm, bf16[32,256,2048]{2,1,0:T(8,128)(2,1)} %get-tuple-element.20.h_hbm, bf16[1536,2048]{1,0:T(8,128)(2,1)} %get-tuple-element.21.w_hbm, f32[32,1,256]{2,1,0:T(1,128)S(1)} %copy-done.2, ...), custom_call_target="tpu_custom_call" | custom-call | tf_op jit(solution)/shard_map/scatter_grads/pallas_call | solution.py:524
  302.3 0.0 copy-done
  302.3 0.0 copy-done.3
  302.3 5.8 %local_backward.1 = (bf16[256,2048]{1,0:T(8,128)(2,1)}, f32[2,1,2176]{2,1,0:T(1,128)S(1)}, f32[2048,1536]{1,0:T(8,128)}) custom-call(f32[256,2048]{1,0:T(8,128)S(1)} %get-tuple-element.24.dh_ref, bf16[256,2048]{1,0:T(8,128)(2,1)S(1)} %bitcast.8, f32[1,2048]{1,0:T(1,128)S(1)} %bitcast.10, f32[16,128]{1,0:T(8,128)S(1)} %get-tuple-element.25.t_ref, ...), custom_call_target="tpu_custom_call" | custom-call | tf_op jit(solution)/shard_map/local_backward/pallas_call | solution.py:584
  308.0 11.1 %group_sums.1 = (f32[1,2048]{1,0:T(1,128)S(1)}, f32[1,2048]{1,0:T(1,128)S(1)}, f32[1,1]{1,0:T(1,128)}) custom-call(f32[2,1,2176]{2,1,0:T(1,128)S(1)} %get-tuple-element.27.mine_ref, f32[32,1,256]{2,1,0:T(1,128)S(1)} %copy-done.2, f32[32,1,512]{2,1,0:T(1,128)S(1)} %copy-done.1), custom_call_target="tpu_custom_call" | custom-call | tf_op jit(solution)/shard_map/group_sums/pallas_call | solution.py:659
  319.7 0.6 copy.15
  320.3 0.6 copy.16
Async XLA Ops:
  118.6 0.8 copy-start.1
  119.4 0.8 copy-start.2
  120.2 182.1 %copy-start = (bf16[8,32,2048]{2,1,0:T(8,128)(2,1)S(1)}, bf16[8,32,2048]{2,1,0:T(8,128)(2,1)}, u32[]{:S(2)}) copy-start(bf16[8,32,2048]{2,1,0:T(8,128)(2,1)} %param.6) | copy-start | bytes 3145732
  120.2 182.1 %copy-start.3 = (f32[2048]{0:T(1024)S(1)}, f32[2048]{0:T(1024)}, u32[]{:S(2)}) copy-start(f32[2048]{0:T(1024)} %param.7) | copy-start | bytes 24580

commit v3 on v2

--- a/solution.py
+++ b/solution.py
@@ -67,8 +67,8 @@
         pl.semaphore_signal(barrier, inc=1, device_id={"vp": lax.rem(me + d, n)}, device_id_type=MESH)
 
 
-def gather_kernel(n, x_ref, gain_ref, bias_ref, tok_ref, w_hbm, h_hbm, z_hbm, wt_hbm, lse_ref, toks_ref,
-                  w_v, wt_v, h_all, zbuf, col, local, got, own, w_sem, wt_sem, h_sem, z_sem, send_x, send_s, send_d, recv_x, recv_s,
+def gather_kernel(n, x_ref, gain_ref, bias_ref, label_ref, mask_ref, w_hbm, h_hbm, z_hbm, wt_hbm, lse_ref, toks_ref,
+                  w_v, wt_v, h_all, zbuf, col, local, got, own, tok_ref, w_sem, wt_sem, h_sem, z_sem, send_x, send_s, send_d, recv_x, recv_s,
                   stat_send, stat_recv, lse_send, lse_recv, tok_send, tok_recv):
     ring = Rings(n)
     me = ring.me
@@ -82,14 +82,16 @@
     w_copy.start()
     signal_all(n, me)
 
-    ln_rows = min(64, rows)
-
-    @pl.loop(0, rows // ln_rows)
-    def _(b):
-        r = pl.ds(pl.multiple_of(b * ln_rows, ln_rows), ln_rows)
-        normed, _ = norm_rows(x_ref[r, :])
-        h_all[0, r, :] = (normed * (1.0 + gain_ref[...]) + bias_ref[...]).astype(BF16)
-
+    ln_rows = min(64, half)
+
+    def norm_half(base):
+        @pl.loop(0, half // ln_rows)
+        def _(b):
+            r = pl.ds(pl.multiple_of(base + b * ln_rows, ln_rows), ln_rows)
+            normed, _ = norm_rows(x_ref[r, :])
+            h_all[0, r, :] = (normed * (1.0 + gain_ref[...]) + bias_ref[...]).astype(BF16)
+
+    norm_half(so)
     pl.semaphore_wait(pltpu.get_barrier_semaphore(), n - 1)
 
     def hop(src, dst, send_sem, recv_sem, who):
@@ -108,6 +110,10 @@
     def d_copy(c, u):
         r = pl.ds(so + (c * quart + u * piece), piece)
         return hop(h_all.at[0, r], h_all.at[n - 1, r], send_d.at[c, u], recv_x.at[n - 1, c, u], ring.sibling)
+
+    for c in range(2):
+        s_copy(0, c, 0).start()
+    norm_half(xo)
 
     def x_arrived(i, c, u):
         r = pl.ds(xo + (c * quart + u * piece), piece)
@@ -165,8 +171,21 @@
     def lse_copy(d):
         return hop(own, lse_ref.at[me], lse_send, lse_recv, lax.rem(me + d, n))
 
-    for c in range(2):
-        s_copy(0, c, 0).start()
+    outer, inner = label_ref.shape
+
+    def in_line(block):
+        lane = lax.broadcasted_iota(jnp.int32, (inner, rows), 1)
+        spread = (lax.rem(lane, inner) == lax.broadcasted_iota(jnp.int32, (inner, rows), 0)).astype(F32)
+        line = lax.div(lax.broadcasted_iota(jnp.int32, (outer, rows), 1), inner)
+        chosen = line == lax.broadcasted_iota(jnp.int32, (outer, rows), 0)
+        return jnp.sum(jnp.where(chosen, jnp.dot(block, spread, preferred_element_type=F32), 0.0), axis=0, keepdims=True)
+
+    def tokens():
+        label = label_ref[...]
+        high = in_line(lax.shift_right_logical(label, 8).astype(F32))
+        tok_ref[:, :rows] = 256.0 * high + in_line((label & 255).astype(F32))
+        tok_ref[:, rows:] = in_line(mask_ref[...])
+
     zbuf[...] = jnp.zeros_like(zbuf)
     w_copy.wait()
 
@@ -206,6 +225,10 @@
                             for v in range(2):
                                 d_copy(c, v).start()
 
+                        tokens()
+
+                    @pl.when(i == 2)
+                    def _():
                         @pl.loop(1, n)
                         def _(d):
                             tok_copy(d).start()
@@ -278,7 +301,7 @@
     lse_total.wait_send()
 
 
-def gather_logits(n, x, gain, bias, toks, w):
+def gather_logits(n, x, gain, bias, labels, mask, w):
     rows, dim = x.shape
     cols = w.shape[1]
     vmem = pl.BlockSpec(memory_space=pltpu.VMEM)
@@ -293,7 +316,7 @@
             jax.ShapeDtypeStruct((n, 1, rows), F32),
             jax.ShapeDtypeStruct((n, 1, 2 * rows), F32),
         ),
-        in_specs=[vmem, vmem, vmem, vmem, hbm],
+        in_specs=[vmem, vmem, vmem, vmem, vmem, hbm],
         out_specs=(hbm, hbm, hbm, vmem, vmem),
         scratch_shapes=[
             pltpu.VMEM((dim, cols), BF16),
@@ -304,12 +327,13 @@
             pltpu.VMEM((n, 2, 1, rows // 2), F32),
             pltpu.VMEM((n, 4, 1, rows // 2), F32),
             pltpu.VMEM((1, rows), F32),
+            pltpu.VMEM((1, 2 * rows), F32),
             dma, dma, dma((2,)), dma((2,)), dma((4, 2, 2)), dma((4, 2, 2)), dma((2, 2)), dma((n, 2, 2)), dma((n, 2, 2)),
             dma, dma, dma, dma, dma, dma,
         ],
         compiler_params=pltpu.CompilerParams(collective_id=0, has_side_effects=True, vmem_limit_bytes=GATHER_VMEM),
         name="gather_logits",
-    )(x, gain.reshape(1, dim), bias.reshape(1, dim), toks, w)
+    )(x, gain.reshape(1, dim), bias.reshape(1, dim), labels, mask, w)
 
 
 SLOTS = 8
@@ -318,8 +342,8 @@
 SCATTER_VMEM = 36_000_000
 
 
-def scatter_kernel(n, z_hbm, h_hbm, w_hbm, lse_ref, toks_ref, dw, dh_ref, t_ref,
-                   w_v, zb, hb, dzb, part, from_x, from_s, from_d, flat, cols, w_sem, z_sem, h_sem,
+def scatter_kernel(n, z_hbm, h_hbm, w_hbm, lse_hbm, toks_hbm, dw, dh_ref, t_ref,
+                   lse_ref, toks_ref, tok_sem, w_v, zb, hb, dzb, part, from_x, from_s, from_d, flat, cols, w_sem, z_sem, h_sem,
                    send_x, send_s, send_d, recv_x, recv_s, recv_d, credit_x, credit_s):
     ring = Rings(n)
     rows, dim = dh_ref.shape
@@ -339,12 +363,18 @@
         ]
 
     w_copy = pltpu.make_async_copy(w_hbm, w_v, w_sem)
-    for copy in fetch(z_hbm, zb, z_sem, 1, 0) + [w_copy] + fetch(h_hbm, hb, h_sem, 1, 0) + fetch(z_hbm, zb, z_sem, 2, 1):
+    tok_copies = [pltpu.make_async_copy(lse_hbm, lse_ref, tok_sem.at[0]), pltpu.make_async_copy(toks_hbm, toks_ref, tok_sem.at[1])]
+    for copy in tok_copies + fetch(z_hbm, zb, z_sem, 1, 0) + [w_copy] + fetch(h_hbm, hb, h_sem, 1, 0) + fetch(z_hbm, zb, z_sem, 2, 1):
         copy.start()
 
+    flat[...] = jnp.zeros_like(flat)
+    dw[...] = jnp.zeros_like(dw)
+    for copy in tok_copies:
+        copy.wait()
     mask_total = jnp.sum(jnp.sum(toks_ref[:, :, rows:], axis=0), axis=-1, keepdims=True)
-    flat[...] = jnp.zeros_like(flat)
-    t_ref[...] = jnp.zeros_like(t_ref)
+    lse_term = jnp.sum(lse_ref[ring.me] * (toks_ref[ring.me][:, rows:] / mask_total), axis=-1, keepdims=True)
+    corner = (lax.broadcasted_iota(jnp.int32, t_ref.shape, 0) == 0) & (lax.broadcasted_iota(jnp.int32, t_ref.shape, 1) == 0)
+    t_ref[...] = jnp.where(corner, -lse_term, 0.0)
 
     def columns(j):
         valid = jnp.where(j <= n, 1.0, 0.0)
@@ -446,7 +476,6 @@
         def _():
             dh_ref[pl.ds(so, half), u * wide:(u + 1) * wide] = part[slot, pl.ds(so, half), :]
 
-    dw[...] = jnp.zeros_like(dw)
     columns(1)
     for copy in fetch(z_hbm, zb, z_sem, 1, 0):
         copy.wait()
@@ -528,9 +557,12 @@
             pltpu.VMEM((rows, dim), F32),
             pltpu.VMEM((16, 128), F32),
         ),
-        in_specs=[hbm, hbm, hbm, vmem, vmem],
+        in_specs=[hbm] * 5,
         out_specs=(vmem, vmem, vmem),
         scratch_shapes=[
+            pltpu.VMEM(lse.shape, F32),
+            pltpu.VMEM(toks.shape, F32),
+            dma((2,)),
             pltpu.VMEM((vocab, dim), BF16),
             pltpu.VMEM((2, rows, vocab), F32),
             pltpu.VMEM((2, rows, dim), BF16),
@@ -548,7 +580,7 @@
         ],
         compiler_params=pltpu.CompilerParams(collective_id=1, has_side_effects=True, vmem_limit_bytes=SCATTER_VMEM),
         name="scatter_grads",
-    )(z, h, w, lse, toks)
+    )(z, h, w, pltpu.with_memory_space_constraint(lse, pltpu.HBM), pltpu.with_memory_space_constraint(toks, pltpu.HBM))
 
 
 def local_kernel(dh_ref, x_ref, gain_ref, t_ref, dw_ref, dx_ref, sums_ref, dw_hbm, dw_sem):
@@ -596,14 +628,13 @@
     )(dh, x, gain.reshape(1, dim), t, dw)
 
 
-def sums_kernel(n, mine_ref, lse_ref, toks_ref, dg_ref, dc_ref, loss_ref,
+def sums_kernel(n, mine_ref, dg_ref, dc_ref, loss_ref,
                 near, both, chips, total, send_a, recv_a, send_b, recv_b, send_c, recv_c):
     me = lax.axis_index("vp")
     core, chip = lax.rem(me, 2), lax.div(me, 2)
     count = n // 2
     sibling = me + 1 - 2 * core
     dim = dg_ref.shape[1]
-    rows = lse_ref.shape[-1]
 
     def peer(d):
         return 2 * lax.rem(chip + d, count) + core
@@ -613,9 +644,6 @@
     for d in range(1, count):
         pl.semaphore_signal(barrier, inc=1, device_id={"vp": peer(d)}, device_id_type=MESH)
 
-    mask = toks_ref[:, :, rows:]
-    mask_total = jnp.sum(jnp.sum(mask, axis=0), axis=-1, keepdims=True)
-    lse_sum = jnp.sum(jnp.sum(lse_ref[...] * (mask / mask_total[None]), axis=0), axis=-1, keepdims=True)
     pl.semaphore_wait(barrier, count)
 
     def hop(src, dst, send_sem, recv_sem, who):
@@ -648,10 +676,10 @@
     third.wait()
     dg_ref[...] = total[0, :, 0:dim]
     dc_ref[...] = total[1, :, 0:dim]
-    loss_ref[...] = lse_sum - jnp.sum(total[0, :, dim:], axis=-1, keepdims=True)
-
-
-def group_sums(n, mine, lse, toks):
+    loss_ref[...] = -jnp.sum(total[0, :, dim:], axis=-1, keepdims=True)
+
+
+def group_sums(n, mine):
     wide = mine.shape[-1]
     dim = wide - 128
     vmem = pl.BlockSpec(memory_space=pltpu.VMEM)
@@ -663,7 +691,7 @@
             jax.ShapeDtypeStruct((1, dim), F32),
             jax.ShapeDtypeStruct((1, 1), F32),
         ),
-        in_specs=[vmem] * 3,
+        in_specs=[vmem],
         out_specs=(vmem,) * 3,
         scratch_shapes=[
             pltpu.VMEM((2, 1, wide), F32),
@@ -674,7 +702,7 @@
         ],
         compiler_params=pltpu.CompilerParams(collective_id=2, has_side_effects=True, vmem_limit_bytes=16_000_000),
         name="group_sums",
-    )(mine, lse, toks)
+    )(mine)
 
 
 def solution(mesh):
@@ -683,12 +711,10 @@
     def per_device(hidden, norm_gain, norm_bias, w_blk, labels, loss_mask):
         dim = hidden.shape[-1]
         x = hidden.reshape(-1, dim)
-        rows = x.shape[0]
-        toks_mine = jnp.concatenate([labels.reshape(1, rows).astype(F32), loss_mask.reshape(1, rows)], axis=1)
-        h, z, wt, lse, toks = gather_logits(n, x, norm_gain, norm_bias, toks_mine, w_blk)
+        h, z, wt, lse, toks = gather_logits(n, x, norm_gain, norm_bias, labels, loss_mask, w_blk)
         dw, dh, t = scatter_grads(n, z, h, wt, lse, toks)
         grad_x, sums, grad_w = local_backward(dh, x, norm_gain, t, dw)
-        grad_gain, grad_bias, loss = group_sums(n, sums, lse, toks)
+        grad_gain, grad_bias, loss = group_sums(n, sums)
         return loss.reshape(1), grad_x.reshape(hidden.shape), grad_w, grad_gain.reshape(dim), grad_bias.reshape(dim)
 
     tok_spec = P("vp", "dp")

time: 322 us -> 318 us (0.988)
  no operation moved by 1% of the time
where the time goes in v3:
time: 318 us; the launch traced here: 317 us
  Pallas kernels  314 us (99%)
    pallas_call x1, Pallas kernels, scatter_grads(): pl.pallas_call(functools.partial(scatter_kernel, n), out_shape=(pltpu.VME...  181 us
    pallas_call x1, Pallas kernels, gather_logits(): pl.pallas_call(functools.partial(gather_kernel, n), out_shape=(jax.ShapeD...  116 us
    pallas_call x1, Pallas kernels, group_sums(): pl.pallas_call(functools.partial(sums_kernel, n), out_shape=(jax.ShapeDty...  11.1 us

profile of v3, /device:TPU:97, one launch (start us, length us, event | category | flops | bytes accessed | tf_op | source)
XLA Modules:
  0.0 317.5 jit_solution(16351556734994396537)
XLA Ops:
  0.6 115.8 %gather_logits.1 = (bf16[32,256,2048]{2,1,0:T(8,128)(2,1)}, f32[32,256,1536]{2,1,0:T(8,128)}, bf16[1536,2048]{1,0:T(8,128)(2,1)}, f32[32,1,256]{2,1,0:T(1,128)}, f32[32,1,512]{2,1,0:T(1,128)}) custom-call(bf16[256,2048]{1,0:T(8,128)(2,1)} %bitcast.7, f32[1,2048]{1,0:T(1,128)} %bitcast.9, f32[1,2048]{1,0:T(1,128)} %bitcast.13, s32[8,32]{1,0:T(8,128)} %label_ref.1, ...), custom_call_target="tpu_custom_call" | custom-call | tf_op jit(solution)/shard_map/gather_logits/pallas_call | solution.py:310
  116.5 0.0 copy-start
  116.5 0.0 copy-start.1
  116.5 181.2 %scatter_grads.1 = (f32[2048,1536]{1,0:T(8,128)S(1)}, f32[256,2048]{1,0:T(8,128)S(1)}, f32[16,128]{1,0:T(8,128)S(1)}) custom-call(f32[32,256,1536]{2,1,0:T(8,128)} %get-tuple-element.19.z_hbm, bf16[32,256,2048]{2,1,0:T(8,128)(2,1)} %get-tuple-element.20.h_hbm, bf16[1536,2048]{1,0:T(8,128)(2,1)} %get-tuple-element.21.w_hbm, ...), custom_call_target="tpu_custom_call" | custom-call | tf_op jit(solution)/shard_map/scatter_grads/pallas_call | solution.py:553
  297.7 0.0 copy-done
  297.7 0.0 copy-done.1
  297.7 5.8 %local_backward.1 = (bf16[256,2048]{1,0:T(8,128)(2,1)}, f32[2,1,2176]{2,1,0:T(1,128)S(1)}, f32[2048,1536]{1,0:T(8,128)}) custom-call(f32[256,2048]{1,0:T(8,128)S(1)} %get-tuple-element.24.dh_ref, bf16[256,2048]{1,0:T(8,128)(2,1)S(1)} %bitcast.8, f32[1,2048]{1,0:T(1,128)S(1)} %bitcast.10, f32[16,128]{1,0:T(8,128)S(1)} %get-tuple-element.25.t_ref, ...), custom_call_target="tpu_custom_call" | custom-call | tf_op jit(solution)/shard_map/local_backward/pallas_call | solution.py:616
  303.4 11.1 %group_sums.1 = (f32[1,2048]{1,0:T(1,128)S(1)}, f32[1,2048]{1,0:T(1,128)S(1)}, f32[1,1]{1,0:T(1,128)}) custom-call(f32[2,1,2176]{2,1,0:T(1,128)S(1)} %get-tuple-element.27.mine_ref), custom_call_target="tpu_custom_call" | custom-call | tf_op jit(solution)/shard_map/group_sums/pallas_call | solution.py:687
  315.1 0.6 copy.15
  315.7 0.6 copy.16
Async XLA Ops:
  116.5 181.2 %copy-start = (bf16[8,32,2048]{2,1,0:T(8,128)(2,1)S(1)}, bf16[8,32,2048]{2,1,0:T(8,128)(2,1)}, u32[]{:S(2)}) copy-start(bf16[8,32,2048]{2,1,0:T(8,128)(2,1)} %param.6) | copy-start | bytes 3145732
  116.5 181.2 %copy-start.1 = (f32[2048]{0:T(1024)S(1)}, f32[2048]{0:T(1024)}, u32[]{:S(2)}) copy-start(f32[2048]{0:T(1024)} %param.7) | copy-start | bytes 24580

commit v4 on v3

--- a/solution.py
+++ b/solution.py
@@ -337,7 +337,7 @@
 
 
 SLOTS = 8
-LAG = 2
+LAG = 1
 PIECES = 4
 SCATTER_VMEM = 36_000_000
 
@@ -583,11 +583,19 @@
     )(z, h, w, pltpu.with_memory_space_constraint(lse, pltpu.HBM), pltpu.with_memory_space_constraint(toks, pltpu.HBM))
 
 
+DW_COPIES = 8
+
+
 def local_kernel(dh_ref, x_ref, gain_ref, t_ref, dw_ref, dx_ref, sums_ref, dw_hbm, dw_sem):
     rows, dim = dh_ref.shape
     blk = min(64, rows)
-    dw_copy = pltpu.make_async_copy(dw_ref, dw_hbm, dw_sem)
-    dw_copy.start()
+    strip = dw_ref.shape[0] // DW_COPIES
+    dw_copies = [
+        pltpu.make_async_copy(dw_ref.at[pl.ds(p * strip, strip)], dw_hbm.at[pl.ds(p * strip, strip)], dw_sem.at[p])
+        for p in range(DW_COPIES)
+    ]
+    for copy in dw_copies:
+        copy.start()
 
     def body(b, carry):
         dg, dc = carry
@@ -607,7 +615,8 @@
     sums_ref[1, :, 0:dim] = dc
     sums_ref[0, :, dim:] = jnp.sum(t_ref[...], axis=0, keepdims=True)
     sums_ref[1, :, dim:] = jnp.zeros((1, 128), F32)
-    dw_copy.wait()
+    for copy in dw_copies:
+        copy.wait()
 
 
 def local_backward(dh, x, gain, t, dw):
@@ -622,7 +631,7 @@
         ),
         in_specs=[vmem] * 5,
         out_specs=(vmem, vmem, pl.BlockSpec(memory_space=pltpu.HBM)),
-        scratch_shapes=[pltpu.SemaphoreType.DMA],
+        scratch_shapes=[pltpu.SemaphoreType.DMA((DW_COPIES,))],
         compiler_params=pltpu.CompilerParams(vmem_limit_bytes=24_000_000),
         name="local_backward",
     )(dh, x, gain.reshape(1, dim), t, dw)

time: 318 us -> 318 us (level)
  no operation moved by 1% of the time
where the time goes in v4:
time: 318 us
  Pallas kernels  314 us (99%)
    pallas_call x1, Pallas kernels, scatter_grads(): pl.pallas_call(functools.partial(scatter_kernel, n), out_shape=(pltpu.VME...  182 us
    pallas_call x1, Pallas kernels, gather_logits(): pl.pallas_call(functools.partial(gather_kernel, n), out_shape=(jax.ShapeD...  116 us
    pallas_call x1, Pallas kernels, group_sums(): pl.pallas_call(functools.partial(sums_kernel, n), out_shape=(jax.ShapeDty...  11.1 us

profile of v4, /device:TPU:97, one launch (start us, length us, event | category | flops | bytes accessed | tf_op | source)
XLA Modules:
  0.0 318.0 jit_solution(6202948607378859797)
XLA Ops:
  0.6 115.8 %gather_logits.1 = (bf16[32,256,2048]{2,1,0:T(8,128)(2,1)}, f32[32,256,1536]{2,1,0:T(8,128)}, bf16[1536,2048]{1,0:T(8,128)(2,1)}, f32[32,1,256]{2,1,0:T(1,128)}, f32[32,1,512]{2,1,0:T(1,128)}) custom-call(bf16[256,2048]{1,0:T(8,128)(2,1)} %bitcast.7, f32[1,2048]{1,0:T(1,128)} %bitcast.9, f32[1,2048]{1,0:T(1,128)} %bitcast.13, s32[8,32]{1,0:T(8,128)} %label_ref.1, ...), custom_call_target="tpu_custom_call" | custom-call | tf_op jit(solution)/shard_map/gather_logits/pallas_call | solution.py:310
  116.5 0.0 copy-start
  116.5 0.0 copy-start.1
  116.5 181.9 %scatter_grads.1 = (f32[2048,1536]{1,0:T(8,128)S(1)}, f32[256,2048]{1,0:T(8,128)S(1)}, f32[16,128]{1,0:T(8,128)S(1)}) custom-call(f32[32,256,1536]{2,1,0:T(8,128)} %get-tuple-element.19.z_hbm, bf16[32,256,2048]{2,1,0:T(8,128)(2,1)} %get-tuple-element.20.h_hbm, bf16[1536,2048]{1,0:T(8,128)(2,1)} %get-tuple-element.21.w_hbm, ...), custom_call_target="tpu_custom_call" | custom-call | tf_op jit(solution)/shard_map/scatter_grads/pallas_call | solution.py:553
  298.4 0.0 copy-done
  298.4 0.0 copy-done.1
  298.4 5.6 %local_backward.1 = (bf16[256,2048]{1,0:T(8,128)(2,1)}, f32[2,1,2176]{2,1,0:T(1,128)S(1)}, f32[2048,1536]{1,0:T(8,128)}) custom-call(f32[256,2048]{1,0:T(8,128)S(1)} %get-tuple-element.24.dh_ref, bf16[256,2048]{1,0:T(8,128)(2,1)S(1)} %bitcast.8, f32[1,2048]{1,0:T(1,128)S(1)} %bitcast.10, f32[16,128]{1,0:T(8,128)S(1)} %get-tuple-element.25.t_ref, ...), custom_call_target="tpu_custom_call" | custom-call | tf_op jit(solution)/shard_map/local_backward/pallas_call | solution.py:625
  304.0 11.1 %group_sums.1 = (f32[1,2048]{1,0:T(1,128)S(1)}, f32[1,2048]{1,0:T(1,128)S(1)}, f32[1,1]{1,0:T(1,128)}) custom-call(f32[2,1,2176]{2,1,0:T(1,128)S(1)} %get-tuple-element.27.mine_ref), custom_call_target="tpu_custom_call" | custom-call | tf_op jit(solution)/shard_map/group_sums/pallas_call | solution.py:696
  315.7 0.6 copy.15
  316.3 0.6 copy.16
Async XLA Ops:
  116.5 181.9 %copy-start = (bf16[8,32,2048]{2,1,0:T(8,128)(2,1)S(1)}, bf16[8,32,2048]{2,1,0:T(8,128)(2,1)}, u32[]{:S(2)}) copy-start(bf16[8,32,2048]{2,1,0:T(8,128)(2,1)} %param.6) | copy-start | bytes 3145732
  116.5 181.9 %copy-start.1 = (f32[2048]{0:T(1024)S(1)}, f32[2048]{0:T(1024)}, u32[]{:S(2)}) copy-start(f32[2048]{0:T(1024)} %param.7) | copy-start | bytes 24580
